TPU v7x, 16 devices: a whole 2x2x2 slice. The times are simulated.
16 devices in a mesh: rep: 1, r: 2 (over z), s: 8 (over x, y, core).
Axes of the slice: x: 2, y: 2, z: 2, core: 2. Of those that a mesh axis runs over, the one named last changes fastest.
Arguments:
- x: bfloat16 [16, 2048, 1024], P(('rep', 'r', 's'))
- dy: bfloat16 [16, 2048, 1024], P(('rep', 'r', 's'))
- w_gate: bfloat16 [2, 1024, 4096], P(None, 's')
- w_up: bfloat16 [2, 1024, 4096], P(None, 's')
- w_down: bfloat16 [2, 4096, 1024], P(None, 's')
Outputs:
- output 1: bfloat16 [16, 2048, 1024], P(('rep', 'r', 's'))
- output 2: bfloat16 [2, 1024, 4096], P('rep', 's')
- output 3: bfloat16 [2, 1024, 4096], P('rep', 's')
- output 4: bfloat16 [2, 4096, 1024], P('rep', 's')
All inputs are finite; a program needn't handle non-finite values.
Results may differ from a plain program's by a relative error of at most 0.018.
Values are sent between devices in bfloat16 or wider.
A program may use at most 2 GiB of HBM per device.

v0:
```python
import jax
import jax.numpy as jnp
from jax import lax
from jax.sharding import PartitionSpec as P

NAMES = ("w_gate", "w_up", "w_down")


def matmul(a, w):
    return jnp.dot(a, w, preferred_element_type=jnp.float32).astype(jnp.bfloat16)


def normed(h):
    wide = h.astype(jnp.float32)
    scale = lax.rsqrt(jnp.mean(wide**2, -1, keepdims=True) + 1e-6)
    return (wide * scale).astype(jnp.bfloat16)


def layer(h, w):
    a = normed(h)
    gate = jnp.dot(a, w["w_gate"], preferred_element_type=jnp.float32)
    up = jnp.dot(a, w["w_up"], preferred_element_type=jnp.float32)
    return h + matmul((jax.nn.silu(gate) * up).astype(jnp.bfloat16), w["w_down"])


def solution(mesh):
    def fetched(weights, number):
        return {name: lax.all_gather(w[number], "s", axis=0, tiled=True) for name, w in zip(NAMES, weights, strict=True)}

    def summed(term):
        return lax.psum(lax.psum_scatter(term, "s", scatter_dimension=0, tiled=True), "r")

    def step(x, dy, *weights):
        layers = weights[0].shape[0]
        h, inputs = x[0], []
        for number in range(layers):
            inputs.append(h)
            h = layer(h, fetched(weights, number))
        by_h, mine = dy[0], [None] * layers
        for number in reversed(range(layers)):
            _, back = jax.vjp(lambda w, h: layer(h, w), fetched(weights, number), inputs[number])
            by_w, by_h = back(by_h)
            mine[number] = [summed(by_w[name]) for name in NAMES]
        return (by_h[None], *(jnp.stack([mine[number][i] for number in range(layers)]) for i in range(3)))

    states, cut = P(("rep", "r", "s"), None, None), P(None, "s", None)
    return jax.shard_map(
        step,
        mesh=mesh,
        in_specs=(states, states) + (cut,) * 3,
        out_specs=(states,) + (P("rep", "s", None),) * 3,
        check_vma=False,
    )
```

profile of v0, /device:TPU:0, one launch (start us, length us, event | category | flops | bytes accessed | tf_op | source)
XLA Modules:
  0.0 1026.2 jit_solution(5271096683366526677)
XLA Ops:
  33.6 29.9 %all-gather.13.cloned.1.call-done = bf16[1,1024,4096]{2,1,0:T(8,128)(2,1)} async-done(((bf16[1,128,4096]{2,1,0:T(8,128)(2,1)}), bf16[1,1024,4096]{2,1,0:T(8,128)(2,1)}) %all-gather.13.cloned.1.call-update) | async-done | bytes 8388624 | tf_op jit(solution)/shard_map/all_gather | solution.py:28
  63.6 24.4 %fusion.37 = f32[2048,4096]{1,0:T(8,128)} fusion(bf16[1,1024,4096]{2,1,0:T(8,128)(2,1)} %all-gather.13.cloned.1.call-done, bf16[1,2048,1024]{1,2,0:T(8,128)(2,1)} %copy.10, f32[2048]{0:T(1024)S(1)} %fusion.61), kind=kOutput, calls=%fused_computation.59 | convolution fusion | flops 17186160640 | bytes 46145536 | tf_op jit(solution)/shard_map/dot_general | solution.py:21
  88.0 27.7 %all-gather.15.cloned.1.call-done = bf16[1,1024,4096]{2,1,0:T(8,128)(2,1)} async-done(((bf16[1,128,4096]{2,1,0:T(8,128)(2,1)}), bf16[1,1024,4096]{2,1,0:T(8,128)(2,1)}) %all-gather.15.cloned.1.call-update) | async-done | bytes 8388624 | tf_op jit(solution)/shard_map/all_gather | solution.py:28
  115.6 39.1 %multiply_convert_fusion.1 = (bf16[2048,4096]{1,0:T(8,128)(2,1)}, f32[2048,4096]{1,0:T(8,128)}) fusion(f32[2048,4096]{1,0:T(8,128)} %fusion.37, bf16[1,1024,4096]{2,1,0:T(8,128)(2,1)} %all-gather.15.cloned.1.call-done, bf16[1,2048,1024]{1,2,0:T(8,128)(2,1)} %copy.10, f32[2048]{0:T(1024)S(1)} %fusion.61), kind=kOutput, calls=%fused_computation.13 | convolution fusion | flops 17236492288 | bytes 96477184 | tf_op jit(solution)/shard_map/dot_general | solution.py:22
  167.6 24.5 %fusion.18 = (f32[2048]{0:T(1024)S(1)}, bf16[2048,1024]{0,1:T(8,128)(2,1)}) fusion(bf16[2048,4096]{1,0:T(8,128)(2,1)} %get-tuple-element.20, bf16[1,4096,1024]{2,1,0:T(8,128)(2,1)} %all-gather.17.cloned.1.call-done, bf16[1,2048,1024]{1,2,0:T(8,128)(2,1)} %copy.10), kind=kOutput, calls=%fused_computation.40 | convolution fusion | flops 17190352896 | bytes 33562624 | tf_op jit(solution)/shard_map/dot_general | solution.py:10
  192.8 27.3 %all-gather.23.cloned.1.call-done = bf16[1,1024,4096]{2,1,0:T(8,128)(2,1)} async-done(((bf16[1,128,4096]{2,1,0:T(8,128)(2,1)}), bf16[1,1024,4096]{2,1,0:T(8,128)(2,1)}) %all-gather.23.cloned.1.call-update) | async-done | bytes 8388624 | tf_op jit(solution)/shard_map/all_gather | solution.py:28
  220.1 24.7 %fusion.21 = f32[2048,4096]{1,0:T(8,128)} fusion(bf16[1,1024,4096]{2,1,0:T(8,128)(2,1)} %all-gather.23.cloned.1.call-done, bf16[2048,1024]{0,1:T(8,128)(2,1)} %get-tuple-element.23, f32[2048]{0:T(1024)S(1)} %fusion.62), kind=kOutput, calls=%fused_computation.43 | convolution fusion | flops 17186160640 | bytes 46145536 | tf_op jit(solution)/shard_map/jvp()/dot_general | solution.py:22
  244.8 27.1 %all-gather.21.cloned.1.call-done = bf16[1,4096,1024]{2,1,0:T(8,128)(2,1)} async-done(((bf16[1,512,1024]{2,1,0:T(8,128)(2,1)}), bf16[1,4096,1024]{2,1,0:T(8,128)(2,1)}) %all-gather.21.cloned.1.call-update) | async-done | bytes 8388624 | tf_op jit(solution)/shard_map/all_gather | solution.py:28
  272.0 24.3 %convolution_convert_fusion.1 = bf16[2048,4096]{1,0:T(8,128)(2,1)} fusion(bf16[1,4096,1024]{2,1,0:T(8,128)(2,1)} %all-gather.21.cloned.1.call-done, bf16[1,2048,1024]{2,1,0:T(8,128)(2,1)} %param.6), kind=kOutput, calls=%fused_computation.22 | convolution fusion | flops 17188257792 | bytes 29360128 | tf_op jit(solution)/shard_map/transpose(jvp())/dot_general | solution.py:10
  296.3 28.2 %all-gather.19.cloned.1.call-done = bf16[1,1024,4096]{2,1,0:T(8,128)(2,1)} async-done(((bf16[1,128,4096]{2,1,0:T(8,128)(2,1)}), bf16[1,1024,4096]{2,1,0:T(8,128)(2,1)}) %all-gather.19.cloned.1.call-update) | async-done | bytes 8388624 | tf_op jit(solution)/shard_map/all_gather | solution.py:28
  324.4 46.7 %fusion.1 = (bf16[2048,4096]{1,0:T(8,128)(2,1)}, f32[2048,4096]{1,0:T(8,128)}) fusion(f32[2048,4096]{1,0:T(8,128)} %fusion.21, bf16[2048,4096]{1,0:T(8,128)(2,1)} %convolution_convert_fusion.1, bf16[1,1024,4096]{2,1,0:T(8,128)(2,1)} %all-gather.19.cloned.1.call-done, bf16[2048,1024]{0,1:T(8,128)(2,1)} %get-tuple-element.23, f32[2048]{0:T(1024)S(1)} %fusion.62), kind=kOutput, calls=%fused_computation.7 | convolution fusion | flops 17286823936 | bytes 113254400 | tf_op jit(solution)/shard_map/jvp()/dot_general | solution.py:21
  371.2 27.1 %fusion.7 = bf16[2048,1024]{0,1:T(8,128)(2,1)} fusion(bf16[2048,4096]{1,0:T(8,128)(2,1)} %convolution_convert_fusion.1, bf16[1,1024,4096]{2,1,0:T(8,128)(2,1)} %all-gather.23.cloned.1.call-done, f32[2048,4096]{1,0:T(8,128)} %get-tuple-element.25), kind=kOutput, calls=%fused_computation.17 | convolution fusion | flops 17230200832 | bytes 62914560 | tf_op jit(solution)/shard_map/transpose(jvp())/dot_general | solution.py:22
  398.3 25.6 %fusion.20 = (f32[2048]{0:T(1024)S(1)}, bf16[2048,1024]{0,1:T(8,128)(2,1)S(1)}) fusion(bf16[2048,1024]{0,1:T(8,128)(2,1)S(1)} %copy-done.5, bf16[2048,1024]{0,1:T(8,128)(2,1)} %fusion.7, bf16[2048,4096]{1,0:T(8,128)(2,1)} %get-tuple-element.24, bf16[1,1024,4096]{2,1,0:T(8,128)(2,1)} %all-gather.19.cloned.1.call-done), kind=kOutput, calls=%fused_computation.42 | convolution fusion | flops 17190352896 | bytes 37756928 | tf_op jit(solution)/shard_map/transpose(jvp())/dot_general | solution.py:21
  452.2 30.7 %fusion.39 = bf16[4096,1024]{1,0:T(8,128)(2,1)} fusion(f32[2048,4096]{1,0:T(8,128)} %fusion.21, bf16[1,2048,1024]{2,1,0:T(8,128)(2,1)} %param.6, f32[2048,4096]{1,0:T(8,128)} %get-tuple-element.25), kind=kOutput, calls=%fused_computation.61 | convolution fusion | flops 17234395136 | bytes 79691776 | tf_op jit(solution)/shard_map/transpose(jvp())/dot_general | solution.py:10
  483.0 46.7 %fusion.3 = (bf16[2048,4096]{1,0:T(8,128)(2,1)}, bf16[2048,4096]{1,0:T(8,128)(2,1)}) fusion(f32[2048,4096]{1,0:T(8,128)} %fusion.37, f32[2048,4096]{1,0:T(8,128)} %get-tuple-element.21, bf16[2048,1024]{0,1:T(8,128)(2,1)} %copy-done.2, bf16[1,4096,1024]{2,1,0:T(8,128)(2,1)} %all-gather.17.cloned.1.call-done), kind=kOutput, calls=%fused_computation.9 | convolution fusion | flops 17288921088 | bytes 113246208 | tf_op jit(solution)/shard_map/transpose(jvp())/dot_general | solution.py:10
  529.7 25.7 %fusion.40 = bf16[1024,4096]{1,0:T(8,128)(2,1)} fusion(bf16[2048,4096]{1,0:T(8,128)(2,1)} %get-tuple-element.29, bf16[1,2048,1024]{1,2,0:T(8,128)(2,1)S(1)} %copy-done, f32[2048]{0:T(1024)S(1)} %copy-done.10, f32[2048,4096]{1,0:T(8,128)} %fusion.37), kind=kOutput, calls=%fused_computation.62 | convolution fusion | flops 17240686592 | bytes 62922752 | tf_op jit(solution)/shard_map/transpose(jvp())/dot_general | solution.py:22
  556.1 26.9 %fusion.41 = bf16[1024,4096]{1,0:T(8,128)(2,1)} fusion(bf16[2048,4096]{1,0:T(8,128)(2,1)} %convolution_convert_fusion.1, bf16[2048,1024]{0,1:T(8,128)(2,1)} %get-tuple-element.23, f32[2048]{0:T(1024)S(1)} %copy-done.12, f32[2048,4096]{1,0:T(8,128)} %get-tuple-element.25), kind=kOutput, calls=%fused_computation.63 | convolution fusion | flops 17240686592 | bytes 62922752 | tf_op jit(solution)/shard_map/transpose(jvp())/dot_general | solution.py:22
  629.2 25.0 %reduce-scatter.11.cloned.1.call-done = bf16[128,4096]{1,0:T(8,128)(2,1)} async-done(((bf16[1024,4096]{1,0:T(8,128)(2,1)}), bf16[128,4096]{1,0:T(8,128)(2,1)}) %reduce-scatter.11.cloned.1.call-update) | async-done | bytes 1048592 | tf_op jit(solution)/shard_map/reduce_scatter | solution.py:31
  654.2 68.3 %reduce-scatter.13.cloned.1.call-done = bf16[128,4096]{1,0:T(8,128)(2,1)} async-done(((bf16[1024,4096]{1,0:T(8,128)(2,1)}), bf16[128,4096]{1,0:T(8,128)(2,1)}) %reduce-scatter.13.cloned.1.call-update) | async-done | bytes 1048592 | tf_op jit(solution)/shard_map/reduce_scatter | solution.py:31
  722.4 68.4 %reduce-scatter.9.cloned.1.call-done = bf16[128,4096]{1,0:T(8,128)(2,1)} async-done(((bf16[1024,4096]{1,0:T(8,128)(2,1)}), bf16[128,4096]{1,0:T(8,128)(2,1)}) %reduce-scatter.9.cloned.1.call-update) | async-done | bytes 1048592 | tf_op jit(solution)/shard_map/reduce_scatter | solution.py:31
  790.9 68.3 %reduce-scatter.7.cloned.1.call-done = bf16[128,4096]{1,0:T(8,128)(2,1)} async-done(((bf16[1024,4096]{1,0:T(8,128)(2,1)}), bf16[128,4096]{1,0:T(8,128)(2,1)}) %reduce-scatter.7.cloned.1.call-update) | async-done | bytes 1048592 | tf_op jit(solution)/shard_map/reduce_scatter | solution.py:31
  859.2 27.4 %fusion.9 = bf16[2048,1024]{0,1:T(8,128)(2,1)} fusion(bf16[2048,4096]{1,0:T(8,128)(2,1)} %get-tuple-element.29, bf16[1,1024,4096]{2,1,0:T(8,128)(2,1)} %all-gather.15.cloned.1.call-done, f32[2048,4096]{1,0:T(8,128)} %fusion.37), kind=kOutput, calls=%fused_computation.19 | convolution fusion | flops 17230200832 | bytes 62914560 | tf_op jit(solution)/shard_map/transpose(jvp())/dot_general | solution.py:22
  886.6 25.1 %fusion.17 = (f32[2048]{0:T(1024)S(1)}, bf16[2048,1024]{0,1:T(8,128)(2,1)S(1)}) fusion(bf16[1,2048,1024]{1,2,0:T(8,128)(2,1)S(1)} %copy-done.1, bf16[2048,1024]{0,1:T(8,128)(2,1)} %fusion.9, bf16[2048,4096]{1,0:T(8,128)(2,1)} %get-tuple-element.28, bf16[1,1024,4096]{2,1,0:T(8,128)(2,1)} %all-gather.13.cloned.1.call-done), kind=kOutput, calls=%fused_computation.39 | convolution fusion | flops 17190352896 | bytes 37756928 | tf_op jit(solution)/shard_map/transpose(jvp())/dot_general | solution.py:21
  922.6 89.0 %all-reduce.3.cloned.1.call-done = (bf16[1,128,4096]{2,1,0:T(8,128)(2,1)}, bf16[1,128,4096]{2,1,0:T(8,128)(2,1)}, bf16[1,128,4096]{2,1,0:T(8,128)(2,1)}, bf16[1,...) async-done(((bf16[1,128,4096]{2,1,0:T(8,128)(2,1)}, bf16[1,128,4096]{2,1,0:T(8,128)(2,1)}, bf16[1,128,4096]{2,1,0:T(8,128)(2,1)}, ...) | async-done | bytes 6291472 | tf_op jit(solution)/shard_map/psum | solution.py:31
  (77 shorter events, 133.5 us)
Async XLA Ops:
  7.2 6.5 copy-start.6
  7.2 56.4 %all-gather.13.cloned.1.call-start = ((), (), s32[]{:S(2)}) async-start(), calls=%async_computation.12 | async-start | bytes 9437184 | tf_op jit(solution)/shard_map/all_gather | solution.py:28
  10.5 105.2 %all-gather.15.cloned.1.call-start = ((), (), s32[]{:S(2)}) async-start(), calls=%async_computation.13 | async-start | bytes 9437184 | tf_op jit(solution)/shard_map/all_gather | solution.py:28
  13.6 154.0 %all-gather.17.cloned.1.call-start = ((), (), s32[]{:S(2)}) async-start(), calls=%async_computation.14 | async-start | bytes 9437184 | tf_op jit(solution)/shard_map/all_gather | solution.py:28
  15.2 204.9 %all-gather.23.cloned.1.call-start = ((), (), s32[]{:S(2)}) async-start(), calls=%async_computation.17 | async-start | bytes 9437184 | tf_op jit(solution)/shard_map/all_gather | solution.py:28
  15.8 256.2 %all-gather.21.cloned.1.call-start = ((), (), s32[]{:S(2)}) async-start(), calls=%async_computation.16 | async-start | bytes 9437184 | tf_op jit(solution)/shard_map/all_gather | solution.py:28
  16.4 308.0 %all-gather.19.cloned.1.call-start = ((), (), s32[]{:S(2)}) async-start(), calls=%async_computation.15 | async-start | bytes 9437184 | tf_op jit(solution)/shard_map/all_gather | solution.py:28
  17.0 612.2 %reduce-scatter.15.cloned.1.call-start = ((), (), s32[]{:S(2)}) async-start(), calls=%async_computation.10 | async-start | bytes 9437184 | tf_op jit(solution)/shard_map/reduce_scatter | solution.py:31
  27.1 88.5 %copy-start.9 = (f32[2048]{0:T(1024)}, f32[2048]{0:T(1024)S(1)}, u32[]{:S(2)}) copy-start(f32[2048]{0:T(1024)S(1)} %fusion.61) | copy-start | bytes 24580
  192.8 231.2 %copy-start.11 = (f32[2048]{0:T(1024)}, f32[2048]{0:T(1024)S(1)}, u32[]{:S(2)}) copy-start(f32[2048]{0:T(1024)S(1)} %fusion.62) | copy-start | bytes 24580
  371.2 27.1 %copy-start.5 = (bf16[2048,1024]{0,1:T(8,128)(2,1)S(1)}, bf16[2048,1024]{0,1:T(8,128)(2,1)}, u32[]{:S(2)}) copy-start(bf16[2048,1024]{0,1:T(8,128)(2,1)} %get-tuple-element.23) | copy-start | bytes 12582916
  398.3 25.6 %copy-start.14 = (f32[2048]{0:T(1024)S(1)}, f32[2048]{0:T(1024)}, u32[]{:S(2)}) copy-start(f32[2048]{0:T(1024)} %copy-done.13) | copy-start | bytes 24580
  398.3 25.6 %copy-start.4 = (bf16[1,2048,1024]{1,2,0:T(8,128)(2,1)S(1)}, bf16[1,2048,1024]{1,2,0:T(8,128)(2,1)}, u32[]{:S(2)}) copy-start(bf16[1,2048,1024]{1,2,0:T(8,128)(2,1)} %copy.9) | copy-start | bytes 12582916
  452.1 177.0 %reduce-scatter.17.cloned.1.call-start = ((), (), s32[]{:S(2)}) async-start(), calls=%async_computation.11 | async-start | bytes 9437184 | tf_op jit(solution)/shard_map/reduce_scatter | solution.py:31
  483.0 171.2 %reduce-scatter.11.cloned.1.call-start = ((), (), s32[]{:S(2)}) async-start(), calls=%async_computation.8 | async-start | bytes 9437184 | tf_op jit(solution)/shard_map/reduce_scatter | solution.py:31
  483.0 46.7 %copy-start = (bf16[1,2048,1024]{1,2,0:T(8,128)(2,1)S(1)}, bf16[1,2048,1024]{1,2,0:T(8,128)(2,1)}, u32[]{:S(2)}) copy-start(bf16[1,2048,1024]{1,2,0:T(8,128)(2,1)} %copy.10) | copy-start | bytes 12582916
  483.0 46.7 %copy-start.10 = (f32[2048]{0:T(1024)S(1)}, f32[2048]{0:T(1024)}, u32[]{:S(2)}) copy-start(f32[2048]{0:T(1024)} %copy-done.9) | copy-start | bytes 24580
  555.4 167.0 %reduce-scatter.13.cloned.1.call-start = ((), (), s32[]{:S(2)}) async-start(), calls=%async_computation.9 | async-start | bytes 9437184 | tf_op jit(solution)/shard_map/reduce_scatter | solution.py:31
  583.1 207.8 %reduce-scatter.9.cloned.1.call-start = ((), (), s32[]{:S(2)}) async-start(), calls=%async_computation.7 | async-start | bytes 9437184 | tf_op jit(solution)/shard_map/reduce_scatter | solution.py:31
  606.1 253.1 %reduce-scatter.7.cloned.1.call-start = ((), (), s32[]{:S(2)}) async-start(), calls=%async_computation.6 | async-start | bytes 9437184 | tf_op jit(solution)/shard_map/reduce_scatter | solution.py:31
  629.1 382.5 %all-reduce.3.cloned.1.call-start = ((), (), s32[]{:S(2)}) async-start(), calls=%async_computation.18 | async-start | bytes 12582912 | tf_op jit(solution)/shard_map/psum | solution.py:31
  859.2 27.4 %copy-start.1 = (bf16[1,2048,1024]{1,2,0:T(8,128)(2,1)S(1)}, bf16[1,2048,1024]{1,2,0:T(8,128)(2,1)}, u32[]{:S(2)}) copy-start(bf16[1,2048,1024]{1,2,0:T(8,128)(2,1)} %copy.10) | copy-start | bytes 12582916
  886.5 25.1 %copy-start.8 = (f32[2048]{0:T(1024)S(1)}, f32[2048]{0:T(1024)}, u32[]{:S(2)}) copy-start(f32[2048]{0:T(1024)} %copy-done.7) | copy-start | bytes 24580
  886.6 25.2 %copy-start.3 = (bf16[2048,1024]{0,1:T(8,128)(2,1)S(1)}, bf16[2048,1024]{0,1:T(8,128)(2,1)}, u32[]{:S(2)}) copy-start(bf16[2048,1024]{0,1:T(8,128)(2,1)} %copy-done.2) | copy-start | bytes 12582916
  (4 other events, 3.9 us)
Sparse Core Ops, SparseCore 0:
  10.6 52.9 all-gather.12
  65.4 50.1 all-gather.14
  117.5 50.1 all-gather.16
  169.9 50.1 all-gather.22
  221.8 50.1 all-gather.20
  274.2 50.1 all-gather.18
  452.3 64.9 reduce-scatter.14
  520.7 64.9 reduce-scatter.16
  589.1 64.9 reduce-scatter.10
  657.4 64.9 reduce-scatter.12
  725.8 64.9 reduce-scatter.8
  794.1 64.9 reduce-scatter.6
  862.2 149.2 all-reduce.2
where the time goes:
time: 1030 us
  matrix products  488 us (47%)
  waiting for transfers between devices  474 us (46%)
  local copies, waits for them, and re-layouts  31 us (3%)
  other arithmetic  18.4 us (2%)
  between operations  14.5 us (1%)
    reduce_scatter x6, waiting for transfers between devices, summed(): lax.psum_scatter(term, 's', scatter_dimension=0, tiled=True)  230 us
    dot_general x6, matrix products, layer(): up = jnp.dot(a, w['w_up'], preferred_element_type=jnp.float32)  171 us
    dot_general x6, matrix products, layer(): gate = jnp.dot(a, w['w_gate'], preferred_element_type=jnp.float32)  168 us
    all_gather x6, waiting for transfers between devices, fetched(): lax.all_gather(w[number], 's', axis=0, tiled=True)  153 us
    dot_general x5, matrix products, matmul(): jnp.dot(a, w, preferred_element_type=jnp.float32).astype(jnp.bfloat16)  149 us
    psum x1, waiting for transfers between devices, summed(): lax.psum(lax.psum_scatter(term, 's', scatter_dimension=0, tiled=True), 'r')  89 us
    unnamed x33, local copies, waits for them, and re-layouts  23.2 us
  transfers between devices with their start and end apart: 13, of which 11 were waited for; matrix products, arithmetic and copies ran while one was open for 39% of the time, Pallas kernels for 0%

commit v1 on v0

v1 whole, which is shorter than its diff:
```python
import functools

import jax
import jax.numpy as jnp
from jax import lax
from jax.experimental import pallas as pl
from jax.experimental.pallas import tpu as pltpu
from jax.sharding import PartitionSpec as P

BF, F32 = jnp.bfloat16, jnp.float32
T, D, FF = 2048, 1024, 4096
TN, TM, MC = 512, 256, 1024
VMEM_LIMIT = 67043328
MESH = pl.DeviceIdType.MESH
DMA = pltpu.SemaphoreType.DMA
ANY = pl.BlockSpec(memory_space=pl.ANY)


def sds(shape, dtype=BF):
    return jax.ShapeDtypeStruct(shape, dtype)


def resident(shape):
    return pl.BlockSpec(shape, lambda i: (0, 0), pipeline_mode=pl.Buffered(1))


def columns(rows, cols):
    return pl.BlockSpec((rows, cols), lambda i: (0, i))


def rows_of(rows, cols):
    return pl.BlockSpec((rows, cols), lambda i: (i, 0))


def dot(a, b, ca=1, cb=0):
    return lax.dot_general(a, b, (((ca,), (cb,)), ((), ())), preferred_element_type=F32)


def chunks(total, size, f):
    def go(i, c):
        f(pl.ds(pl.multiple_of(i * size, size), size))
        return c

    lax.fori_loop(0, total // size, go, 0)


class Place:
    def __init__(self):
        self.rep, self.r, self.s = lax.axis_index("rep"), lax.axis_index("r"), lax.axis_index("s")
        s = self.s
        x, y, c = s // 4, (s // 2) % 2, s % 2
        at = lambda x, y, c: x * 4 + y * 2 + c
        self.sx, self.sy, self.sd, self.sc = at(1 - x, y, c), at(x, 1 - y, c), at(1 - x, 1 - y, c), at(x, y, 1 - c)
        self.order = [self.sd, self.sx, self.sy, s]
        self.across = [at(1 - x, 1 - y, 1 - c), at(1 - x, y, 1 - c), at(x, 1 - y, 1 - c), self.sc]
        self.dev = {
            "x": (self.rep, self.r, self.sx),
            "y": (self.rep, self.r, self.sy),
            "z": (self.rep, 1 - self.r, s),
            "c": (self.rep, self.r, self.sc),
        }

    def meet(self):
        barrier = pltpu.get_barrier_semaphore()
        for d in "xyzc":
            pl.semaphore_signal(barrier, inc=1, device_id=self.dev[d], device_id_type=MESH)
        pl.semaphore_wait(barrier, 4)


def rows_at(start, size, unit):
    return pl.ds(pl.multiple_of(start, unit), size)


class Gather:
    TAGS = 17

    def __init__(self, shards, layers, steps):
        self.ins, self.layers, self.steps, n = list(shards), layers, steps, len(shards)
        self.n = n
        self.outs = [sds((8 * a.shape[1], a.shape[2])) for a in shards]
        self.scratch = [pltpu.VMEM(a.shape[1:], BF) for a in shards]
        self.scratch += [DMA((n, 2)), DMA((n, self.TAGS)), DMA((n, self.TAGS))]

    def hooks(self, place, ins, outs, scratch):
        own, (local, send, recv) = scratch[: self.n], scratch[self.n :]
        p = place

        def moves(i):
            shard, whole, layer = ins[i], outs[i], self.layers[i]
            rows = shard.shape[1]
            n = rows // 4
            q = [k + p.r * (3 - 2 * k) for k in range(4)]
            slot = lambda owner, k: whole.at[rows_at(owner * rows + q[k] * n, n, n)]
            three = lambda owner: whole.at[rows_at(owner * rows + p.r * n, 3 * n, n)]
            direct = shard.at[layer, rows_at(p.r * n, 3 * n, n)]
            mine = whole.at[rows_at(p.s * rows, rows, rows)]
            todo = [(direct, three(p.s), "x"), (direct, three(p.s), "y")]
            relay = [(slot(p.sy, 0), "x"), (slot(p.sx, 1), "y"), (slot(p.sx, 0), "z"), (slot(p.sy, 0), "z")]
            relay += [(slot(p.sd, 0), "z"), (slot(p.sd, 1), "z")]
            todo += [(a, a, d) for a, d in relay]
            todo += [(shard.at[layer], mine, "c")]
            core = [three(p.sx), three(p.sy), slot(p.sd, 0), slot(p.sd, 1)]
            core += [slot(p.sx, 3), slot(p.sy, 3), slot(p.sd, 3), slot(p.sd, 2)]
            todo += [(a, a, "c") for a in core]
            def move(t):
                a, b, d = todo[t]
                return pltpu.make_async_remote_copy(a, b, send.at[i, t], recv.at[i, t], device_id=p.dev[d], device_id_type=MESH)

            load = lambda: pltpu.make_async_copy(shard.at[layer], own[i], local.at[i, 0])
            save = lambda: pltpu.make_async_copy(own[i], mine, local.at[i, 1])
            return move, load, save

        def a0(i):
            m, load, _ = moves(i)
            for t in (0, 1, 8):
                m(t).start()
            load().start()

        def a1(i):
            m, load, save = moves(i)
            m(0).wait_recv()
            m(3).start()
            m(4).start()
            m(1).wait_recv()
            for t in (2, 5, 9, 10):
                m(t).start()
            load().wait()
            save().start()

        def a2(i):
            m, _, _ = moves(i)
            m(2).wait_recv()
            m(6).start()
            m(11).start()
            m(3).wait_recv()
            m(7).start()
            m(12).start()

        def a3(i):
            m, _, _ = moves(i)
            for t, u in ((4, 13), (5, 14), (6, 15), (7, 16)):
                m(t).wait_recv()
                m(u).start()

        def a4(i):
            m, _, save = moves(i)
            for t in range(8, 17):
                m(t).wait_recv()
            for t in range(17):
                m(t).wait_send()
            save().wait()

        stage = [a0, a1, a2, a3, a4]
        return [(at, functools.partial(stage[k], i)) for at, k, i in self.steps]


def gather_steps(n, at):
    out = [(at(0), 0, i) for i in range(min(2, n))]
    for k in range(n + 3):
        if 0 <= k < n:
            out.append((at(k + 1), 1, k))
            if k + 2 < n:
                out.append((at(k + 1), 0, k + 2))
        if 0 <= k - 1 < n:
            out.append((at(k + 1), 2, k - 1))
        if 0 <= k - 2 < n:
            out.append((at(k + 1), 3, k - 2))
        if 0 <= k - 3 < n:
            out.append((at(k + 1), 4, k - 3))
    return out


def added(out, *terms):
    rows, cols = out.shape
    size = 65536 // cols

    def one(m):
        total = terms[0][m, :].astype(F32)
        for t in terms[1:]:
            total += t[m, :].astype(F32)
        out[m, :] = total.astype(BF)

    chunks(rows, size, one)


class Scatter:
    def __init__(self, term, at, finish=False):
        self.rows, self.cols = term.shape[0] // 8, term.shape[1]
        self.ins, self.at, self.finish = [term], at, finish
        self.outs = [sds((self.rows, self.cols))]
        block, half = (self.rows, self.cols), (self.rows // 2, self.cols)
        self.scratch = [pltpu.VMEM((4, *block), BF), pltpu.VMEM((4, *block), BF), pltpu.VMEM((2, *half), BF), pltpu.VMEM((2, *block), BF)]
        self.scratch += [DMA((5,)), DMA((11,)), DMA((11,))]
        if finish:
            self.scratch.append(pltpu.VMEM(block, BF))

    def hooks(self, place, ins, outs, scratch):
        p, (term,), (result,) = place, ins, outs
        own, other, diag, side, local, send, recv = scratch[:7]
        rows, h = self.rows, self.rows // 2
        block = lambda b: term.at[rows_at(b * rows, rows, rows)]
        part = lambda ref, k, j: ref.at[k, pl.ds(j * h, h)]

        def move(t, a, b, d):
            return pltpu.make_async_remote_copy(a, b, send.at[t], recv.at[t], device_id=p.dev[d], device_id_type=MESH)

        swap = lambda k: move(k, block(p.across[k]), other.at[k], "c")
        load = lambda k: pltpu.make_async_copy(block(p.order[k]), own.at[k], local.at[k])
        corner = lambda j: move(4 + j, part(other, 0, j), diag.at[j], "xy"[j])
        edge = lambda k, j: move(6 + 2 * k + j, part(other, 1 + k, j), part(side, k, j), "xy"[k])

        def r0():
            for k in range(4):
                swap(k).start()
                load(k).start()

        def ready(k):
            swap(k).wait_recv()
            load(k).wait()

        def r1():
            ready(0)
            for j in range(2):
                added(part(other, 0, j), part(other, 0, j), part(own, 0, j))
                corner(j).start()

        def r2():
            for k in range(2):
                ready(1 + k)
                added(part(other, 1 + k, k), part(other, 1 + k, k), part(own, 1 + k, k))
                edge(k, k).start()

        def r3():
            for k in range(2):
                j = 1 - k
                corner(j).wait_recv()
                added(part(other, 1 + k, j), part(other, 1 + k, j), part(own, 1 + k, j), diag.at[j])
                edge(k, j).start()

        def r4():
            ready(3)
            for k in range(2):
                for j in range(2):
                    edge(k, j).wait_recv()
            added(own.at[0], own.at[3], other.at[3], side.at[0], side.at[1])
            for k in range(4):
                swap(k).wait_send()
            for j in range(2):
                corner(j).wait_send()
            for k in range(2):
                for j in range(2):
                    edge(k, j).wait_send()
            if self.finish:
                far = scratch[7]
                over = move(10, own.at[0], far, "z")
                over.start()
                over.wait()
                added(own.at[1], own.at[0], far)
                save = pltpu.make_async_copy(own.at[1], result, local.at[4])
            else:
                save = pltpu.make_async_copy(own.at[0], result, local.at[4])
            save.start()
            save.wait()

        return list(zip(self.at, (r0, r1, r2, r3, r4)))


class Cross:
    def __init__(self, block, at):
        self.ins, self.outs, self.at = [block], [sds(block.shape)], at
        self.scratch = [pltpu.VMEM(block.shape, BF), pltpu.VMEM(block.shape, BF), DMA((2,)), DMA((1,)), DMA((1,))]

    def hooks(self, place, ins, outs, scratch):
        (block,), (result,), (mine, far, local, send, recv) = ins, outs, scratch
        over = lambda: pltpu.make_async_remote_copy(block, far, send.at[0], recv.at[0], device_id=place.dev["z"], device_id_type=MESH)
        load = lambda: pltpu.make_async_copy(block, mine, local.at[0])
        save = lambda: pltpu.make_async_copy(mine, result, local.at[1])

        def z0():
            over().start()
            load().start()

        def z1():
            load().wait()
            over().wait()
            added(mine, mine, far)
            save().start()
            save().wait()

        return list(zip(self.at, (z0, z1)))


def call(number, body, steps, ins, outs, args, scratch=(), comms=()):
    sizes = [(len(c.ins), len(c.outs), len(c.scratch)) for c in comms]
    nin, nout, nscr = len(ins), len(outs), len(scratch)

    def kernel(*refs):
        refs = list(refs)

        def take(n):
            got = refs[:n]
            del refs[:n]
            return got

        main_in = take(nin)
        c_in = [take(a) for a, _, _ in sizes]
        main_out = take(nout)
        c_out = [take(b) for _, b, _ in sizes]
        main_scr = take(nscr)
        c_scr = [take(c) for _, _, c in sizes]
        todo = []
        step = pl.program_id(0)
        if comms:
            place = Place()

            @pl.when(step == 0)
            def _():
                place.meet()

            for c, i, o, s in zip(comms, c_in, c_out, c_scr):
                todo += c.hooks(place, i, o, s)
        for k in range(steps):
            now = [f for at, f in todo if at == k]
            if now:

                @pl.when(step == k)
                def _(now=now):
                    for f in now:
                        f()

        if body is not None:
            body(*main_in, *main_out, *main_scr)
        last = [f for at, f in todo if at >= steps]
        if last:

            @pl.when(step == steps - 1)
            def _():
                for f in last:
                    f()

    c_args = [a for c in comms for a in c.ins]
    c_outs = [o for c in comms for o in c.outs]
    extra = dict(collective_id=number, has_side_effects=True) if comms else {}
    out = pl.pallas_call(
        kernel,
        grid=(steps,),
        in_specs=[*ins, *[ANY] * len(c_args)],
        out_specs=[*[o for o, _ in outs], *[ANY] * len(c_outs)],
        out_shape=[*[s for _, s in outs], *c_outs],
        scratch_shapes=[*scratch, *[s for c in comms for s in c.scratch]],
        compiler_params=pltpu.CompilerParams(vmem_limit_bytes=VMEM_LIMIT, dimension_semantics=("arbitrary",), **extra),
    )(*args, *c_args)
    return out[:nout], out[nout:]


def norm_tile(h):
    wide = h.astype(F32)
    scale = lax.rsqrt(jnp.mean(wide * wide, -1, keepdims=True) + 1e-6)
    return (wide * scale).astype(BF)


def up_body(x, wg, wu, a, gate, up, hidden):
    @pl.when(pl.program_id(0) == 0)
    def _():
        def one(m):
            a[m, :] = norm_tile(x[m, :])

        chunks(T, 256, one)

    def one(m):
        g, u = dot(a[m, :], wg[...]), dot(a[m, :], wu[...])
        gate[m, :], up[m, :] = g, u
        hidden[m, :] = (g * jax.nn.sigmoid(g) * u).astype(BF)

    chunks(T, MC, one)


def down_body(hidden, wd, x, h, a):
    new = x[...] + dot(hidden[...], wd[...]).astype(BF)
    h[...] = new
    a[...] = norm_tile(new)


def gates(g, u, dh):
    sig = jax.nn.sigmoid(g)
    return (dh * u * (sig * (1 + g * (1 - sig)))).astype(BF), (dh * (g * sig)).astype(BF)


def top_body(a, dy, wg, wu, wd, hidden, dgate, dup):
    def one(m):
        g, u = dot(a[m, :], wg[...]), dot(a[m, :], wu[...])
        dh = dot(dy[m, :], wd[...], 1, 1).astype(BF).astype(F32)
        hidden[m, :] = (g * jax.nn.sigmoid(g) * u).astype(BF)
        dgate[m, :], dup[m, :] = gates(g, u, dh)

    chunks(T, MC, one)


def wdown_body(hidden, dy, out):
    out[...] = dot(hidden[...], dy[...], 0, 0).astype(BF)


def low_body(dy, wd, gate, up, hidden, dgate, dup, out):
    def one(m):
        dh = dot(dy[m, :], wd[...], 1, 1).astype(BF).astype(F32)
        dgate[m, :], dup[m, :] = gates(gate[m, :], up[m, :], dh)

    chunks(T, MC, one)
    out[...] = dot(hidden[...], dy[...], 0, 0).astype(BF)


def wide_body(a, dgate, dup, og, ou, at):
    @pl.when(pl.program_id(0) == 0)
    def _():
        def one(m):
            at[:, m] = a[m, :].T

        chunks(T, 256, one)

    og[...] = dot(at[...], dgate[...]).astype(BF)
    ou[...] = dot(at[...], dup[...]).astype(BF)


def back_body(dgate, dup, wg, wu, h, dy, out):
    da = dot(dgate[...], wg[...], 1, 1) + dot(dup[...], wu[...], 1, 1)
    wide = h[...].astype(F32)
    scale = lax.rsqrt(jnp.mean(wide * wide, -1, keepdims=True) + 1e-6)
    inner = jnp.mean(da * wide, -1, keepdims=True)
    dh = scale * da - wide * (scale * scale * scale * inner)
    out[...] = (dy[...].astype(F32) + dh.astype(BF).astype(F32)).astype(BF)


def k_up(number, x, wg, wu, comms):
    wide = columns(T, TN)
    outs = [(resident((T, D)), sds((T, D))), (wide, sds((T, FF), F32)), (wide, sds((T, FF), F32)), (wide, sds((T, FF)))]
    return call(number, up_body, FF // TN, [resident((T, D)), columns(D, TN), columns(D, TN)], outs, (x, wg, wu), comms=comms)


def k_down(number, hidden, wd, x, comms):
    r = rows_of(TM, D)
    outs = [(r, sds((T, D))), (r, sds((T, D)))]
    return call(number, down_body, T // TM, [rows_of(TM, FF), resident((FF, D)), r], outs, (hidden, wd, x), comms=comms)


def k_top(number, a, dy, wg, wu, wd, comms):
    wide = columns(T, TN)
    ins = [resident((T, D)), resident((T, D)), columns(D, TN), columns(D, TN), rows_of(TN, D)]
    return call(number, top_body, FF // TN, ins, [(wide, sds((T, FF)))] * 3, (a, dy, wg, wu, wd), comms=comms)


def k_wdown(number, hidden, dy, comms):
    return call(number, wdown_body, FF // TN, [columns(T, TN), resident((T, D))], [(rows_of(TN, D), sds((FF, D)))], (hidden, dy), comms=comms)


def k_low(number, dy, wd, gate, up, hidden, comms):
    wide = columns(T, TN)
    ins = [resident((T, D)), rows_of(TN, D), wide, wide, wide]
    outs = [(wide, sds((T, FF))), (wide, sds((T, FF))), (rows_of(TN, D), sds((FF, D)))]
    return call(number, low_body, FF // TN, ins, outs, (dy, wd, gate, up, hidden), comms=comms)


def k_wide(number, a, dgate, dup, comms):
    ins = [resident((T, D)), columns(T, TN), columns(T, TN)]
    outs = [(columns(D, TN), sds((D, FF)))] * 2
    return call(number, wide_body, FF // TN, ins, outs, (a, dgate, dup), [pltpu.VMEM((D, T), BF)], comms=comms)


def k_back(number, dgate, dup, wg, wu, h, dy, comms):
    r = rows_of(TM, D)
    ins = [rows_of(TM, FF), rows_of(TM, FF), resident((D, FF)), resident((D, FF)), r, r]
    return call(number, back_body, T // TM, ins, [(r, sds((T, D)))], (dgate, dup, wg, wu, h, dy), comms=comms)


def k_comm(number, comms):
    return call(number, None, 1, [], [], (), comms=comms)[1]


SCATTER_AT = (0, 1, 2, 4, 8)
CROSS_AT = (0, 6)


def solution(mesh):
    def step(x, dy, wg, wu, wd):
        x, dy = x[0], dy[0]
        wg0, wu0 = k_comm(0, [Gather([wg, wu], [0, 0], gather_steps(2, lambda k: 0))])
        fetch = Gather([wd, wg, wu], [0, 1, 1], gather_steps(3, lambda k: (0, 2, 3, 5, 6, 8, 8)[k]))
        (a0, gate, up, hidden), (wd0, wg1, wu1) = k_up(1, x, wg0, wu0, [fetch])
        fetch = Gather([wd], [1], gather_steps(1, lambda k: (0, 6, 8, 8, 8)[k]))
        (h1, a1), (wd1,) = k_down(2, hidden, wd0, x, [fetch])
        (top, dgate, dup), _ = k_top(3, a1, dy, wg1, wu1, wd1, [])
        (td1,), _ = k_wdown(4, top, dy, [])
        (tg1, tu1), (pd1,) = k_wide(5, a1, dgate, dup, [Scatter(td1, SCATTER_AT)])
        (dh,), (pg1, od1) = k_back(6, dgate, dup, wg1, wu1, h1, dy, [Scatter(tg1, SCATTER_AT), Cross(pd1, CROSS_AT)])
        (dgate, dup, td0), (pu1, og1) = k_low(7, dh, wd0, gate, up, hidden, [Scatter(tu1, SCATTER_AT), Cross(pg1, CROSS_AT)])
        (tg0, tu0), (pd0, ou1) = k_wide(8, a0, dgate, dup, [Scatter(td0, SCATTER_AT), Cross(pu1, CROSS_AT)])
        (dx,), (pg0, od0) = k_back(9, dgate, dup, wg0, wu0, x, dh, [Scatter(tg0, SCATTER_AT), Cross(pd0, CROSS_AT)])
        ou0, og0 = k_comm(10, [Scatter(tu0, (0,) * 5, finish=True), Cross(pg0, (0, 0))])
        return dx[None], jnp.stack([og0, og1]), jnp.stack([ou0, ou1]), jnp.stack([od0, od1])

    states, cut = P(("rep", "r", "s"), None, None), P(None, "s", None)
    return jax.shard_map(
        step,
        mesh=mesh,
        in_specs=(states, states) + (cut,) * 3,
        out_specs=(states,) + (P("rep", "s", None),) * 3,
        check_vma=False,
    )
```

time: 1030 us -> 696 us (0.68)
  Pallas kernels: 0 us -> 686 us
  matrix products: 488 us -> 0 us
  waiting for transfers between devices: 474 us -> 0 us
  local copies, waits for them, and re-layouts: 31 us -> 3.46 us
  between operations: 14.5 us -> 0.72 us
  other arithmetic: 18.4 us -> 6.21 us
    pallas_call x0 -> x11, Pallas kernels: none -> 686 us  [call(): pl.pallas_call(kernel, grid=(steps,), in_specs=[*ins, *[ANY] * len(c_args...]
    dot_general x17 -> x0, matrix products: 488 us -> none  [the longest x6 171 us: layer(): up = jnp.dot(a, w['w_up'], preferred_element_type=jnp.float32)]
    reduce_scatter x6 -> x0, waiting for transfers between devices: 230 us -> none  [summed(): lax.psum_scatter(term, 's', scatter_dimension=0, tiled=True)]
    all_gather x6 -> x0, waiting for transfers between devices: 153 us -> none  [fetched(): lax.all_gather(w[number], 's', axis=0, tiled=True)]
    psum x1 -> x0, waiting for transfers between devices: 89 us -> none  [summed(): lax.psum(lax.psum_scatter(term, 's', scatter_dimension=0, tiled=True), 'r')]
    unnamed x33 -> x7, local copies, waits for them, and re-layouts: 23.2 us -> 3.46 us
  transfers between devices with their start and end apart: 13 -> 0, of which waited for: 11 -> 0; matrix products, arithmetic and copies ran while one was open for 39% -> 0% of each run, Pallas kernels for 0% -> 0%
where the time goes in v1:
time: 696 us
  Pallas kernels  686 us (99%)
    pallas_call x11, Pallas kernels, call(): pl.pallas_call(kernel, grid=(steps,), in_specs=[*ins, *[ANY] * len(c_args...  686 us

profile of v1, /device:TPU:0, one launch (start us, length us, event | category | flops | bytes accessed | tf_op | source)
XLA Modules:
  0.0 696.0 jit_solution(6645111757193939518)
XLA Ops:
  0.6 75.9 %shard_map.84 = (bf16[1024,4096]{1,0:T(8,128)(2,1)}, bf16[1024,4096]{1,0:T(8,128)(2,1)}) custom-call(bf16[2,128,4096]{2,1,0:T(8,128)(2,1)} %refs_4_.1, bf16[2,128,4096]{2,1,0:T(8,128)(2,1)} %refs_5_.1), custom_call_target="tpu_custom_call" | custom-call | tf_op jit(solution)/shard_map/pallas_call | solution.py:344
  76.6 105.1 %shard_map.85 = (bf16[2048,1024]{1,0:T(8,128)(2,1)}, f32[2048,4096]{1,0:T(8,128)}, f32[2048,4096]{1,0:T(8,128)}, bf16[2048,4096]{1,0:T(8,128)(2,1)}, bf16[4096,1...) custom-call(bf16[2048,1024]{1,0:T(8,128)(2,1)} %bitcast.9, ...), custom_call_target="tpu_custom_call" | custom-call | tf_op jit(solution)/shard_map/pallas_call | solution.py:344
  181.7 50.8 %shard_map.86 = (bf16[2048,1024]{1,0:T(8,128)(2,1)}, bf16[2048,1024]{1,0:T(8,128)(2,1)}, bf16[4096,1024]{1,0:T(8,128)(2,1)}) custom-call(bf16[2048,4096]{1,0:T(8,128)(2,1)} %get-tuple-element.41.refs_0_.refs_4_, bf16[4096,1024]{1,0:T(8,128)(2,1)} %get-tuple-element.42.refs_1_, bf16[2048,1024]{1,0:T(8,128)(2,1)} %bitcast.10, bf16[2,512,1024]{2,1,0:T(8,128)(2,1)} %refs_3_.3), custom_call_target="tpu_custom_call" | custom-call | tf_op jit(solution)/shard_map/pallas_call | solution.py:344
  232.6 65.4 %shard_map.87 = (bf16[2048,4096]{1,0:T(8,128)(2,1)}, bf16[2048,4096]{1,0:T(8,128)(2,1)}, bf16[2048,4096]{1,0:T(8,128)(2,1)}) custom-call(bf16[2048,1024]{1,0:T(8,128)(2,1)} %get-tuple-element.43.refs_0_, bf16[2048,1024]{1,0:T(8,128)(2,1)} %bitcast.12, bf16[1024,4096]{1,0:T(8,128)(2,1)} %get-tuple-element.44.refs_2_, ...), custom_call_target="tpu_custom_call" | custom-call | tf_op jit(solution)/shard_map/pallas_call | solution.py:344
  298.0 22.8 %shard_map.88.refs_3_ = bf16[4096,1024]{1,0:T(8,128)(2,1)} custom-call(bf16[2048,4096]{1,0:T(8,128)(2,1)} %get-tuple-element.50.refs_0_, bf16[2048,1024]{1,0:T(8,128)(2,1)} %bitcast.13), custom_call_target="tpu_custom_call" | custom-call | tf_op jit(solution)/shard_map/pallas_call | solution.py:344
  320.7 49.8 %shard_map.89 = (bf16[1024,4096]{1,0:T(8,128)(2,1)}, bf16[1024,4096]{1,0:T(8,128)(2,1)}, bf16[512,1024]{1,0:T(8,128)(2,1)}) custom-call(bf16[2048,1024]{1,0:T(8,128)(2,1)} %get-tuple-element.43.refs_0_, bf16[2048,4096]{1,0:T(8,128)(2,1)} %get-tuple-element.47.refs_1_.refs_0_, bf16[2048,4096]{1,0:T(8,128)(2,1)} %get-tuple-element.48.refs_2_.refs_1_, ...), custom_call_target="tpu_custom_call" | custom-call | tf_op jit(solution)/shard_map/pallas_call | solution.py:344
  370.6 54.0 %shard_map.90 = (bf16[2048,1024]{1,0:T(8,128)(2,1)}, bf16[128,4096]{1,0:T(8,128)(2,1)}, bf16[512,1024]{1,0:T(8,128)(2,1)}) custom-call(bf16[2048,4096]{1,0:T(8,128)(2,1)} %get-tuple-element.47.refs_1_.refs_0_, bf16[2048,4096]{1,0:T(8,128)(2,1)} %get-tuple-element.48.refs_2_.refs_1_, bf16[1024,4096]{1,0:T(8,128)(2,1)} %get-tuple-element.44.refs_2_, ...), custom_call_target="tpu_custom_call" | custom-call | tf_op jit(solution)/shard_map/pallas_call | solution.py:344
  424.5 67.7 %shard_map.91 = (bf16[2048,4096]{1,0:T(8,128)(2,1)}, bf16[2048,4096]{1,0:T(8,128)(2,1)}, bf16[4096,1024]{1,0:T(8,128)(2,1)}, bf16[128,4096]{1,0:T(8,128)(2,1)}, bf16[128,4096]{1,0:T(8,128)(2,1)}) custom-call(bf16[2048,1024]{1,0:T(8,128)(2,1)} %get-tuple-element.53.refs_0_.refs_5_, bf16[4096,1024]{1,0:T(8,128)(2,1)} %get-tuple-element.42.refs_1_, ...), custom_call_target="tpu_custom_call" | custom-call | tf_op jit(solution)/shard_map/pallas_call | solution.py:344
  492.3 49.7 %shard_map.92 = (bf16[1024,4096]{1,0:T(8,128)(2,1)}, bf16[1024,4096]{1,0:T(8,128)(2,1)}, bf16[512,1024]{1,0:T(8,128)(2,1)}, bf16[128,4096]{1,0:T(8,128)(2,1)}) custom-call(bf16[2048,1024]{1,0:T(8,128)(2,1)} %get-tuple-element.60.refs_0_, bf16[2048,4096]{1,0:T(8,128)(2,1)} %get-tuple-element.58.refs_1_.refs_0_, ...), custom_call_target="tpu_custom_call" | custom-call | tf_op jit(solution)/shard_map/pallas_call | solution.py:344
  542.0 53.2 %shard_map.93 = (bf16[2048,1024]{1,0:T(8,128)(2,1)}, bf16[128,4096]{1,0:T(8,128)(2,1)}, bf16[512,1024]{1,0:T(8,128)(2,1)}) custom-call(bf16[2048,4096]{1,0:T(8,128)(2,1)} %get-tuple-element.58.refs_1_.refs_0_, bf16[2048,4096]{1,0:T(8,128)(2,1)} %get-tuple-element.59.refs_2_.refs_1_, bf16[1024,4096]{1,0:T(8,128)(2,1)} %get-tuple-element.39.refs_1_.refs_2_, ...), custom_call_target="tpu_custom_call" | custom-call | tf_op jit(solution)/shard_map/pallas_call | solution.py:344
  595.2 91.0 %shard_map.94 = (bf16[128,4096]{1,0:T(8,128)(2,1)}, bf16[128,4096]{1,0:T(8,128)(2,1)}) custom-call(bf16[1024,4096]{1,0:T(8,128)(2,1)} %get-tuple-element.66.refs_0_, bf16[128,4096]{1,0:T(8,128)(2,1)} %get-tuple-element.67.refs_1_), custom_call_target="tpu_custom_call" | custom-call | tf_op jit(solution)/shard_map/pallas_call | solution.py:344
  686.3 0.0 copy-start.1
  686.3 0.0 copy-start.2
  686.3 4.7 pad_maximum_fusion
  691.0 0.0 copy-start
  691.0 0.0 copy-done.1
  691.0 0.0 copy-done.2
  691.0 1.5 pad_maximum_fusion.2
  692.5 1.4 copy-done
  694.0 2.0 copy.10
Async XLA Ops:
  686.3 4.7 copy-start.1
  686.3 4.7 copy-start.2
  691.0 2.9 copy-start

commit v2 on v1

--- a/solution.py
+++ b/solution.py
@@ -72,42 +72,51 @@
 
 
 class Gather:
-    TAGS = 17
-
-    def __init__(self, shards, layers, steps):
-        self.ins, self.layers, self.steps, n = list(shards), layers, steps, len(shards)
-        self.n = n
+    TAGS, PARTS = 17, 2
+
+    def __init__(self, shards, layers, at):
+        self.ins, self.layers, n = list(shards), layers, len(shards)
         self.outs = [sds((8 * a.shape[1], a.shape[2])) for a in shards]
-        self.scratch = [pltpu.VMEM(a.shape[1:], BF) for a in shards]
-        self.scratch += [DMA((n, 2)), DMA((n, self.TAGS)), DMA((n, self.TAGS))]
+        self.work = [(i, k) for i in range(0, n) for k in range(self.PARTS)]
+        self.at, count = at, len(shards) * self.PARTS
+        self.scratch = [pltpu.VMEM((a.shape[1], a.shape[2] // self.PARTS), BF) for a in shards for _ in range(self.PARTS)]
+        self.scratch += [DMA((count, 2)), DMA((count, self.TAGS)), DMA((count, self.TAGS))]
+
+    def reorder(self, work):
+        self.work = work
+        return self
 
     def hooks(self, place, ins, outs, scratch):
-        own, (local, send, recv) = scratch[: self.n], scratch[self.n :]
-        p = place
-
-        def moves(i):
-            shard, whole, layer = ins[i], outs[i], self.layers[i]
+        p, count = place, len(self.work)
+        bounce, (local, send, recv) = scratch[:count], scratch[count:]
+
+        def moves(w):
+            i, k = self.work[w]
+            layer, width = self.layers[i], ins[i].shape[2] // self.PARTS
+            over = pl.ds(k * width, width)
+            shard, whole, own = ins[i], outs[i], bounce[i * self.PARTS + k]
             rows = shard.shape[1]
             n = rows // 4
             q = [k + p.r * (3 - 2 * k) for k in range(4)]
-            slot = lambda owner, k: whole.at[rows_at(owner * rows + q[k] * n, n, n)]
-            three = lambda owner: whole.at[rows_at(owner * rows + p.r * n, 3 * n, n)]
-            direct = shard.at[layer, rows_at(p.r * n, 3 * n, n)]
-            mine = whole.at[rows_at(p.s * rows, rows, rows)]
+            slot = lambda owner, k: whole.at[rows_at(owner * rows + q[k] * n, n, n), over]
+            three = lambda owner: whole.at[rows_at(owner * rows + p.r * n, 3 * n, n), over]
+            direct = shard.at[layer, rows_at(p.r * n, 3 * n, n), over]
+            all_mine, mine = shard.at[layer, :, over], whole.at[rows_at(p.s * rows, rows, rows), over]
             todo = [(direct, three(p.s), "x"), (direct, three(p.s), "y")]
             relay = [(slot(p.sy, 0), "x"), (slot(p.sx, 1), "y"), (slot(p.sx, 0), "z"), (slot(p.sy, 0), "z")]
             relay += [(slot(p.sd, 0), "z"), (slot(p.sd, 1), "z")]
             todo += [(a, a, d) for a, d in relay]
-            todo += [(shard.at[layer], mine, "c")]
+            todo += [(all_mine, mine, "c")]
             core = [three(p.sx), three(p.sy), slot(p.sd, 0), slot(p.sd, 1)]
             core += [slot(p.sx, 3), slot(p.sy, 3), slot(p.sd, 3), slot(p.sd, 2)]
             todo += [(a, a, "c") for a in core]
+
             def move(t):
                 a, b, d = todo[t]
-                return pltpu.make_async_remote_copy(a, b, send.at[i, t], recv.at[i, t], device_id=p.dev[d], device_id_type=MESH)
-
-            load = lambda: pltpu.make_async_copy(shard.at[layer], own[i], local.at[i, 0])
-            save = lambda: pltpu.make_async_copy(own[i], mine, local.at[i, 1])
+                return pltpu.make_async_remote_copy(a, b, send.at[w, t], recv.at[w, t], device_id=p.dev[d], device_id_type=MESH)
+
+            load = lambda: pltpu.make_async_copy(all_mine, own, local.at[w, 0])
+            save = lambda: pltpu.make_async_copy(own, mine, local.at[w, 1])
             return move, load, save
 
         def a0(i):
@@ -150,24 +159,20 @@
                 m(t).wait_send()
             save().wait()
 
-        stage = [a0, a1, a2, a3, a4]
-        return [(at, functools.partial(stage[k], i)) for at, k, i in self.steps]
-
-
-def gather_steps(n, at):
-    out = [(at(0), 0, i) for i in range(min(2, n))]
-    for k in range(n + 3):
-        if 0 <= k < n:
-            out.append((at(k + 1), 1, k))
-            if k + 2 < n:
-                out.append((at(k + 1), 0, k + 2))
-        if 0 <= k - 1 < n:
-            out.append((at(k + 1), 2, k - 1))
-        if 0 <= k - 2 < n:
-            out.append((at(k + 1), 3, k - 2))
-        if 0 <= k - 3 < n:
-            out.append((at(k + 1), 4, k - 3))
-    return out
+        ahead, out = 3, []
+
+        def add(at, f, i):
+            if 0 <= i < count:
+                out.append((at, functools.partial(f, i)))
+
+        for i in range(ahead):
+            add(0, a0, i)
+        for k in range(count + 3):
+            at = self.at(k)
+            for f, i in ((a1, k), (a0, k + ahead), (a2, k - 1), (a3, k - 2), (a4, k - 3)):
+                if f is not a0 or i >= ahead:
+                    add(at, f, i)
+        return out
 
 
 def added(out, *terms):
@@ -184,8 +189,8 @@
 
 
 class Scatter:
-    def __init__(self, term, at, finish=False):
-        self.rows, self.cols = term.shape[0] // 8, term.shape[1]
+    def __init__(self, term, at, finish=False, part=(0, 1)):
+        self.rows, self.cols, self.first = term.shape[0] // 8, term.shape[1] // part[1], term.shape[1] // part[1] * part[0]
         self.ins, self.at, self.finish = [term], at, finish
         self.outs = [sds((self.rows, self.cols))]
         block, half = (self.rows, self.cols), (self.rows // 2, self.cols)
@@ -198,7 +203,7 @@
         p, (term,), (result,) = place, ins, outs
         own, other, diag, side, local, send, recv = scratch[:7]
         rows, h = self.rows, self.rows // 2
-        block = lambda b: term.at[rows_at(b * rows, rows, rows)]
+        block = lambda b: term.at[rows_at(b * rows, rows, rows), pl.ds(self.first, self.cols)]
         part = lambda ref, k, j: ref.at[k, pl.ds(j * h, h)]
 
         def move(t, a, b, d):
@@ -208,6 +213,8 @@
         load = lambda k: pltpu.make_async_copy(block(p.order[k]), own.at[k], local.at[k])
         corner = lambda j: move(4 + j, part(other, 0, j), diag.at[j], "xy"[j])
         edge = lambda k, j: move(6 + 2 * k + j, part(other, 1 + k, j), part(side, k, j), "xy"[k])
+        over = lambda: move(10, own.at[0], scratch[7], "z")
+        save = lambda k: pltpu.make_async_copy(own.at[k], result, local.at[4])
 
         def r0():
             for k in range(4):
@@ -243,6 +250,10 @@
                 for j in range(2):
                     edge(k, j).wait_recv()
             added(own.at[0], own.at[3], other.at[3], side.at[0], side.at[1])
+            if self.finish:
+                over().start()
+            else:
+                save(0).start()
             for k in range(4):
                 swap(k).wait_send()
             for j in range(2):
@@ -250,19 +261,17 @@
             for k in range(2):
                 for j in range(2):
                     edge(k, j).wait_send()
+
+        def r5():
             if self.finish:
-                far = scratch[7]
-                over = move(10, own.at[0], far, "z")
-                over.start()
-                over.wait()
-                added(own.at[1], own.at[0], far)
-                save = pltpu.make_async_copy(own.at[1], result, local.at[4])
-            else:
-                save = pltpu.make_async_copy(own.at[0], result, local.at[4])
-            save.start()
-            save.wait()
-
-        return list(zip(self.at, (r0, r1, r2, r3, r4)))
+                over().wait()
+                added(own.at[1], own.at[0], scratch[7])
+                save(1).start()
+
+        def r6():
+            save(0).wait()
+
+        return list(zip(self.at, (r0, r1, r2, r3, r4, r5, r6)))
 
 
 class Cross:
@@ -290,7 +299,7 @@
         return list(zip(self.at, (z0, z1)))
 
 
-def call(number, body, steps, ins, outs, args, scratch=(), comms=()):
+def call(number, body, steps, ins, outs, args, scratch=(), comms=(), share=False):
     sizes = [(len(c.ins), len(c.outs), len(c.scratch)) for c in comms]
     nin, nout, nscr = len(ins), len(outs), len(scratch)
 
@@ -319,8 +328,9 @@
 
             for c, i, o, s in zip(comms, c_in, c_out, c_scr):
                 todo += c.hooks(place, i, o, s)
+        todo.sort(key=lambda t: t[0])
         for k in range(steps):
-            now = [f for at, f in todo if at == k]
+            now = [f for at, f in todo if k <= at < k + 1]
             if now:
 
                 @pl.when(step == k)
@@ -329,7 +339,7 @@
                         f()
 
         if body is not None:
-            body(*main_in, *main_out, *main_scr)
+            body(*main_in, *main_out, *main_scr, *([c_out[0]] if share else []))
         last = [f for at, f in todo if at >= steps]
         if last:
 
@@ -359,26 +369,61 @@
     return (wide * scale).astype(BF)
 
 
-def up_body(x, wg, wu, a, gate, up, hidden):
-    @pl.when(pl.program_id(0) == 0)
+UT = 256
+UPS = FF // UT
+
+
+def first_body(x, a, gate, up, hidden, h, a1, g_buf, u_buf, kept, wd, sems, wd_sem, wholes):
+    step = pl.program_id(0)
+    fetch = lambda tile: [
+        pltpu.make_async_copy(whole.at[:, rows_at(tile * UT, UT, UT)], buf.at[tile % 2], sems.at[k, tile % 2])
+        for k, (whole, buf) in enumerate(((wholes[0], g_buf), (wholes[1], u_buf)))
+    ]
+    fetch_down = lambda: pltpu.make_async_copy(wholes[2], wd, wd_sem.at[0])
+
+    @pl.when(step == 0)
     def _():
+        for c in fetch(0):
+            c.start()
+
         def one(m):
             a[m, :] = norm_tile(x[m, :])
 
         chunks(T, 256, one)
 
-    def one(m):
-        g, u = dot(a[m, :], wg[...]), dot(a[m, :], wu[...])
-        gate[m, :], up[m, :] = g, u
-        hidden[m, :] = (g * jax.nn.sigmoid(g) * u).astype(BF)
-
-    chunks(T, MC, one)
-
-
-def down_body(hidden, wd, x, h, a):
-    new = x[...] + dot(hidden[...], wd[...]).astype(BF)
-    h[...] = new
-    a[...] = norm_tile(new)
+    @pl.when(step < UPS)
+    def _():
+        for c in fetch(step):
+            c.wait()
+
+        @pl.when(step < UPS - 1)
+        def _():
+            for c in fetch(step + 1):
+                c.start()
+
+        @pl.when(step == UPS - 1)
+        def _():
+            fetch_down().start()
+
+        def one(m):
+            g, u = dot(a[m, :], g_buf[step % 2]), dot(a[m, :], u_buf[step % 2])
+            gate[m, :], up[m, :] = g, u
+            made = (g * jax.nn.sigmoid(g) * u).astype(BF)
+            hidden[m, :] = made
+            kept[m, rows_at(step * UT, UT, UT)] = made
+
+        chunks(T, MC, one)
+
+    @pl.when(step == UPS)
+    def _():
+        fetch_down().wait()
+
+    @pl.when(step >= UPS)
+    def _():
+        m = rows_at((step - UPS) * TM, TM, TM)
+        new = x[m, :] + dot(kept[m, :], wd[...]).astype(BF)
+        h[...] = new
+        a1[...] = norm_tile(new)
 
 
 def gates(g, u, dh):
@@ -430,16 +475,13 @@
     out[...] = (dy[...].astype(F32) + dh.astype(BF).astype(F32)).astype(BF)
 
 
-def k_up(number, x, wg, wu, comms):
-    wide = columns(T, TN)
+def k_first(number, x, gather):
+    wide = pl.BlockSpec((T, UT), lambda i: (0, jnp.minimum(i, UPS - 1)))
+    r = pl.BlockSpec((TM, D), lambda i: (jnp.maximum(i - UPS, 0), 0))
     outs = [(resident((T, D)), sds((T, D))), (wide, sds((T, FF), F32)), (wide, sds((T, FF), F32)), (wide, sds((T, FF)))]
-    return call(number, up_body, FF // TN, [resident((T, D)), columns(D, TN), columns(D, TN)], outs, (x, wg, wu), comms=comms)
-
-
-def k_down(number, hidden, wd, x, comms):
-    r = rows_of(TM, D)
-    outs = [(r, sds((T, D))), (r, sds((T, D)))]
-    return call(number, down_body, T // TM, [rows_of(TM, FF), resident((FF, D)), r], outs, (hidden, wd, x), comms=comms)
+    outs += [(r, sds((T, D))), (r, sds((T, D)))]
+    scratch = [pltpu.VMEM((2, D, UT), BF), pltpu.VMEM((2, D, UT), BF), pltpu.VMEM((T, FF), BF), pltpu.VMEM((FF, D), BF), DMA((2, 2)), DMA((1,))]
+    return call(number, first_body, UPS + T // TM, [resident((T, D))], outs, (x,), scratch, comms=[gather], share=True)
 
 
 def k_top(number, a, dy, wg, wu, wd, comms):
@@ -475,26 +517,31 @@
     return call(number, None, 1, [], [], (), comms=comms)[1]
 
 
-SCATTER_AT = (0, 1, 2, 4, 8)
+SCATTER_AT = (0, 1, 2, 4, 8, 8, 8)
 CROSS_AT = (0, 6)
 
 
 def solution(mesh):
     def step(x, dy, wg, wu, wd):
         x, dy = x[0], dy[0]
-        wg0, wu0 = k_comm(0, [Gather([wg, wu], [0, 0], gather_steps(2, lambda k: 0))])
-        fetch = Gather([wd, wg, wu], [0, 1, 1], gather_steps(3, lambda k: (0, 2, 3, 5, 6, 8, 8)[k]))
-        (a0, gate, up, hidden), (wd0, wg1, wu1) = k_up(1, x, wg0, wu0, [fetch])
-        fetch = Gather([wd], [1], gather_steps(1, lambda k: (0, 6, 8, 8, 8)[k]))
-        (h1, a1), (wd1,) = k_down(2, hidden, wd0, x, [fetch])
+        when = (0, 0, 0, 0, 0, 3, 6, 9, 12, 15, 18, 21, 24, 24.1, 24.2)
+        gather = Gather([wg, wu, wd, wg, wu, wd], [0, 0, 0, 1, 1, 1], lambda k: when[k])
+        gather.reorder([(0, 0), (1, 0), (0, 1), (1, 1), *[(i, k) for i in range(2, 6) for k in range(2)]])
+        (a0, gate, up, hidden, h1, a1), (wg0, wu0, wd0, wg1, wu1, wd1) = k_first(0, x, gather)
         (top, dgate, dup), _ = k_top(3, a1, dy, wg1, wu1, wd1, [])
         (td1,), _ = k_wdown(4, top, dy, [])
         (tg1, tu1), (pd1,) = k_wide(5, a1, dgate, dup, [Scatter(td1, SCATTER_AT)])
         (dh,), (pg1, od1) = k_back(6, dgate, dup, wg1, wu1, h1, dy, [Scatter(tg1, SCATTER_AT), Cross(pd1, CROSS_AT)])
         (dgate, dup, td0), (pu1, og1) = k_low(7, dh, wd0, gate, up, hidden, [Scatter(tu1, SCATTER_AT), Cross(pg1, CROSS_AT)])
         (tg0, tu0), (pd0, ou1) = k_wide(8, a0, dgate, dup, [Scatter(td0, SCATTER_AT), Cross(pu1, CROSS_AT)])
-        (dx,), (pg0, od0) = k_back(9, dgate, dup, wg0, wu0, x, dh, [Scatter(tg0, SCATTER_AT), Cross(pd0, CROSS_AT)])
-        ou0, og0 = k_comm(10, [Scatter(tu0, (0,) * 5, finish=True), Cross(pg0, (0, 0))])
+        last = [
+            Cross(pd0, CROSS_AT),
+            Scatter(tg0, (0, 1, 1.1, 3, 7, 8.25, 8.7), True),
+            Scatter(tu0, (1.2, 4, 4.1, 8, 8.2, 8.4, 8.8), True, (0, 2)),
+            Scatter(tu0, (2, 5, 8.05, 8.1, 8.3, 8.5, 8.9), True, (1, 2)),
+        ]
+        (dx,), (od0, og0, *ou0) = k_back(9, dgate, dup, wg0, wu0, x, dh, last)
+        ou0 = jnp.concatenate(ou0, 1)
         return dx[None], jnp.stack([og0, og1]), jnp.stack([ou0, ou1]), jnp.stack([od0, od1])
 
     states, cut = P(("rep", "r", "s"), None, None), P(None, "s", None)

time: 696 us -> 593 us (0.85)
  Pallas kernels: 686 us -> 582 us
    pallas_call x11 -> x8, Pallas kernels: 686 us -> 582 us  [call(): pl.pallas_call(kernel, grid=(steps,), in_specs=[*ins, *[ANY] * len(c_args...]
where the time goes in v2:
time: 593 us
  Pallas kernels  582 us (98%)
  other arithmetic  7.18 us (1%)
    pallas_call x8, Pallas kernels, call(): pl.pallas_call(kernel, grid=(steps,), in_specs=[*ins, *[ANY] * len(c_args...  582 us

profile of v2, /device:TPU:0, one launch (start us, length us, event | category | flops | bytes accessed | tf_op | source)
XLA Modules:
  0.0 593.2 jit_solution(11032531566191947072)
XLA Ops:
  0.6 173.5 %shard_map.84 = (bf16[2048,1024]{1,0:T(8,128)(2,1)}, f32[2048,4096]{1,0:T(8,128)}, f32[2048,4096]{1,0:T(8,128)}, bf16[2048,4096]{1,0:T(8,128)(2,1)}, bf16[2048,1...) custom-call(bf16[2048,1024]{1,0:T(8,128)(2,1)} %bitcast.13, ...), custom_call_target="tpu_custom_call" | custom-call | tf_op jit(solution)/shard_map/pallas_call | solution.py:354
  174.2 65.4 %shard_map.85 = (bf16[2048,4096]{1,0:T(8,128)(2,1)}, bf16[2048,4096]{1,0:T(8,128)(2,1)}, bf16[2048,4096]{1,0:T(8,128)(2,1)}) custom-call(bf16[2048,1024]{1,0:T(8,128)(2,1)} %get-tuple-element.39.refs_0_, bf16[2048,1024]{1,0:T(8,128)(2,1)} %bitcast.10, bf16[1024,4096]{1,0:T(8,128)(2,1)} %get-tuple-element.40.refs_2_, ...), custom_call_target="tpu_custom_call" | custom-call | tf_op jit(solution)/shard_map/pallas_call | solution.py:354
  239.6 22.8 %shard_map.86.refs_3_ = bf16[4096,1024]{1,0:T(8,128)(2,1)} custom-call(bf16[2048,4096]{1,0:T(8,128)(2,1)} %get-tuple-element.46.refs_0_, bf16[2048,1024]{1,0:T(8,128)(2,1)} %bitcast.11), custom_call_target="tpu_custom_call" | custom-call | tf_op jit(solution)/shard_map/pallas_call | solution.py:354
  262.4 49.7 %shard_map.87 = (bf16[1024,4096]{1,0:T(8,128)(2,1)}, bf16[1024,4096]{1,0:T(8,128)(2,1)}, bf16[512,1024]{1,0:T(8,128)(2,1)}) custom-call(bf16[2048,1024]{1,0:T(8,128)(2,1)} %get-tuple-element.39.refs_0_, bf16[2048,4096]{1,0:T(8,128)(2,1)} %get-tuple-element.43.refs_1_.refs_0_, bf16[2048,4096]{1,0:T(8,128)(2,1)} %get-tuple-element.44.refs_2_.refs_1_, ...), custom_call_target="tpu_custom_call" | custom-call | tf_op jit(solution)/shard_map/pallas_call | solution.py:354
  312.1 53.7 %shard_map.88 = (bf16[2048,1024]{1,0:T(8,128)(2,1)}, bf16[128,4096]{1,0:T(8,128)(2,1)}, bf16[512,1024]{1,0:T(8,128)(2,1)}) custom-call(bf16[2048,4096]{1,0:T(8,128)(2,1)} %get-tuple-element.43.refs_1_.refs_0_, bf16[2048,4096]{1,0:T(8,128)(2,1)} %get-tuple-element.44.refs_2_.refs_1_, bf16[1024,4096]{1,0:T(8,128)(2,1)} %get-tuple-element.40.refs_2_, ...), custom_call_target="tpu_custom_call" | custom-call | tf_op jit(solution)/shard_map/pallas_call | solution.py:354
  365.9 67.8 %shard_map.89 = (bf16[2048,4096]{1,0:T(8,128)(2,1)}, bf16[2048,4096]{1,0:T(8,128)(2,1)}, bf16[4096,1024]{1,0:T(8,128)(2,1)}, bf16[128,4096]{1,0:T(8,128)(2,1)}, bf16[128,4096]{1,0:T(8,128)(2,1)}) custom-call(bf16[2048,1024]{1,0:T(8,128)(2,1)} %get-tuple-element.49.refs_0_.refs_5_, bf16[4096,1024]{1,0:T(8,128)(2,1)} %get-tuple-element.50.refs_1_, ...), custom_call_target="tpu_custom_call" | custom-call | tf_op jit(solution)/shard_map/pallas_call | solution.py:354
  433.7 49.9 %shard_map.90 = (bf16[1024,4096]{1,0:T(8,128)(2,1)}, bf16[1024,4096]{1,0:T(8,128)(2,1)}, bf16[512,1024]{1,0:T(8,128)(2,1)}, bf16[128,4096]{1,0:T(8,128)(2,1)}) custom-call(bf16[2048,1024]{1,0:T(8,128)(2,1)} %get-tuple-element.60.refs_0_, bf16[2048,4096]{1,0:T(8,128)(2,1)} %get-tuple-element.56.refs_1_.refs_0_, ...), custom_call_target="tpu_custom_call" | custom-call | tf_op jit(solution)/shard_map/pallas_call | solution.py:354
  483.6 98.9 %shard_map.91 = (bf16[2048,1024]{1,0:T(8,128)(2,1)}, bf16[512,1024]{1,0:T(8,128)(2,1)}, bf16[128,4096]{1,0:T(8,128)(2,1)}, bf16[128,2048]{1,0:T(8,128)(2,1)}, bf16[128,2048]{1,0:T(8,128)(2,1)}) custom-call(bf16[2048,4096]{1,0:T(8,128)(2,1)} %get-tuple-element.56.refs_1_.refs_0_, bf16[2048,4096]{1,0:T(8,128)(2,1)} %get-tuple-element.57.refs_2_.refs_1_, ...), custom_call_target="tpu_custom_call" | custom-call | tf_op jit(solution)/shard_map/pallas_call | solution.py:354
  582.6 1.3 maximum_bitcast_fusion
  583.9 0.0 copy-start.1
  583.9 0.0 copy-start.2
  583.9 4.4 pad_maximum_fusion
  588.3 0.0 copy-start
  588.3 0.0 copy-done.1
  588.3 0.0 copy-done.2
  588.3 1.5 pad_maximum_fusion.2
  589.8 1.4 copy-done
  591.2 2.0 copy.10
Async XLA Ops:
  583.9 4.4 copy-start.1
  583.9 4.4 copy-start.2
  588.3 2.9 copy-start

commit v3 on v2

--- a/solution.py
+++ b/solution.py
@@ -11,6 +11,7 @@
 T, D, FF = 2048, 1024, 4096
 TN, TM, MC = 512, 256, 1024
 VMEM_LIMIT = 67043328
+AHEAD, LAGS, PARTS = 3, (2, 4, 6), 4
 MESH = pl.DeviceIdType.MESH
 DMA = pltpu.SemaphoreType.DMA
 ANY = pl.BlockSpec(memory_space=pl.ANY)
@@ -72,15 +73,14 @@
 
 
 class Gather:
-    TAGS, PARTS = 17, 2
+    TAGS, PARTS = 18, PARTS
 
     def __init__(self, shards, layers, at):
         self.ins, self.layers, n = list(shards), layers, len(shards)
         self.outs = [sds((8 * a.shape[1], a.shape[2])) for a in shards]
         self.work = [(i, k) for i in range(0, n) for k in range(self.PARTS)]
         self.at, count = at, len(shards) * self.PARTS
-        self.scratch = [pltpu.VMEM((a.shape[1], a.shape[2] // self.PARTS), BF) for a in shards for _ in range(self.PARTS)]
-        self.scratch += [DMA((count, 2)), DMA((count, self.TAGS)), DMA((count, self.TAGS))]
+        self.scratch = [DMA((count, self.TAGS)), DMA((count, self.TAGS))]
 
     def reorder(self, work):
         self.work = work
@@ -88,13 +88,13 @@
 
     def hooks(self, place, ins, outs, scratch):
         p, count = place, len(self.work)
-        bounce, (local, send, recv) = scratch[:count], scratch[count:]
+        send, recv = scratch
 
         def moves(w):
             i, k = self.work[w]
             layer, width = self.layers[i], ins[i].shape[2] // self.PARTS
             over = pl.ds(k * width, width)
-            shard, whole, own = ins[i], outs[i], bounce[i * self.PARTS + k]
+            shard, whole = ins[i], outs[i]
             rows = shard.shape[1]
             n = rows // 4
             q = [k + p.r * (3 - 2 * k) for k in range(4)]
@@ -109,35 +109,33 @@
             todo += [(all_mine, mine, "c")]
             core = [three(p.sx), three(p.sy), slot(p.sd, 0), slot(p.sd, 1)]
             core += [slot(p.sx, 3), slot(p.sy, 3), slot(p.sd, 3), slot(p.sd, 2)]
-            todo += [(a, a, "c") for a in core]
+            theirs = whole.at[rows_at(p.sc * rows, rows, rows), over]
+            todo += [(a, a, "c") for a in [*core, theirs]]
 
             def move(t):
                 a, b, d = todo[t]
                 return pltpu.make_async_remote_copy(a, b, send.at[w, t], recv.at[w, t], device_id=p.dev[d], device_id_type=MESH)
 
-            load = lambda: pltpu.make_async_copy(all_mine, own, local.at[w, 0])
-            save = lambda: pltpu.make_async_copy(own, mine, local.at[w, 1])
-            return move, load, save
+            return move
 
         def a0(i):
-            m, load, _ = moves(i)
+            m = moves(i)
             for t in (0, 1, 8):
                 m(t).start()
-            load().start()
 
         def a1(i):
-            m, load, save = moves(i)
+            m = moves(i)
             m(0).wait_recv()
             m(3).start()
             m(4).start()
             m(1).wait_recv()
             for t in (2, 5, 9, 10):
                 m(t).start()
-            load().wait()
-            save().start()
+            m(8).wait_recv()
+            m(17).start()
 
         def a2(i):
-            m, _, _ = moves(i)
+            m = moves(i)
             m(2).wait_recv()
             m(6).start()
             m(11).start()
@@ -146,33 +144,51 @@
             m(12).start()
 
         def a3(i):
-            m, _, _ = moves(i)
+            m = moves(i)
             for t, u in ((4, 13), (5, 14), (6, 15), (7, 16)):
                 m(t).wait_recv()
                 m(u).start()
 
         def a4(i):
-            m, _, save = moves(i)
-            for t in range(8, 17):
+            m = moves(i)
+            for t in range(9, 18):
                 m(t).wait_recv()
-            for t in range(17):
+            for t in range(18):
                 m(t).wait_send()
-            save().wait()
-
-        ahead, out = 3, []
+
+        out = []
 
         def add(at, f, i):
             if 0 <= i < count:
                 out.append((at, functools.partial(f, i)))
 
-        for i in range(ahead):
+        for i in range(AHEAD):
             add(0, a0, i)
-        for k in range(count + 3):
-            at = self.at(k)
-            for f, i in ((a1, k), (a0, k + ahead), (a2, k - 1), (a3, k - 2), (a4, k - 3)):
-                if f is not a0 or i >= ahead:
-                    add(at, f, i)
+        for k in range(count + LAGS[2]):
+            at = self.at[k]
+            add(at, a1, k)
+            add(at, a0, k + AHEAD)
+            for f, lag in zip((a2, a3, a4), LAGS):
+                add(at, f, k - lag)
         return out
+
+
+def gather_times():
+    work = [(m, k) for pair in ((0, 1), (2,), (5,), (3, 4)) for k in range(PARTS) for m in pair]
+    one, each = 22.5 / PARTS, UPS // PARTS
+    first = one * (2 + LAGS[2]) + 8
+    starts = [first + 3.5 * min(i, UPS) + 3 * min(max(i - UPS, 0), DOWNS) + 5.2 * max(i - TOP, 0) for i in range(TOP + UPS)]
+    need = {0: lambda k: max(each * k - 1, 0), 1: lambda k: max(each * k - 1, 0), 2: lambda k: UPS - 1, 5: lambda k: TOP}
+    need[3] = need[4] = lambda k: TOP + max(each * k - 1, 0)
+    total, when, cap = len(work) + LAGS[2], [], TOP + UPS - 1
+    for k in reversed(range(total)):
+        if k >= LAGS[2]:
+            m, part = work[k - LAGS[2]]
+            cap = min(cap, need[m](part))
+        arrives = one * (k + 1) + 8
+        late = [i for i, t in enumerate(starts) if t >= arrives - 1]
+        when.append(min([cap, *late[:1]]))
+    return work, when[::-1]
 
 
 def added(out, *terms):
@@ -299,7 +315,7 @@
         return list(zip(self.at, (z0, z1)))
 
 
-def call(number, body, steps, ins, outs, args, scratch=(), comms=(), share=False):
+def call(number, body, steps, ins, outs, args, scratch=(), comms=(), share=False, early=None):
     sizes = [(len(c.ins), len(c.outs), len(c.scratch)) for c in comms]
     nin, nout, nscr = len(ins), len(outs), len(scratch)
 
@@ -319,6 +335,12 @@
         c_scr = [take(c) for _, _, c in sizes]
         todo = []
         step = pl.program_id(0)
+        if early is not None:
+
+            @pl.when(step == 0)
+            def _():
+                early(*main_in, *main_out, *main_scr)
+
         if comms:
             place = Place()
 
@@ -370,36 +392,51 @@
 
 
 UT = 256
-UPS = FF // UT
-
-
-def first_body(x, a, gate, up, hidden, h, a1, g_buf, u_buf, kept, wd, sems, wd_sem, wholes):
+UPS, DOWNS = FF // UT, T // TM
+TOP = UPS + DOWNS
+
+
+def first_body(x, dy, a, gate, up, hidden, h, a1, dgate, dup, td, g_buf, u_buf, kept, wd, states, made, sems, one_sem, wholes):
     step = pl.program_id(0)
-    fetch = lambda tile: [
-        pltpu.make_async_copy(whole.at[:, rows_at(tile * UT, UT, UT)], buf.at[tile % 2], sems.at[k, tile % 2])
-        for k, (whole, buf) in enumerate(((wholes[0], g_buf), (wholes[1], u_buf)))
-    ]
-    fetch_down = lambda: pltpu.make_async_copy(wholes[2], wd, wd_sem.at[0])
+
+    def tile_of(k, tile):
+        cols = rows_at(tile * UT, UT, UT)
+        pairs = [(wholes[k].at[:, cols], g_buf), (wholes[k + 1].at[:, cols], u_buf)]
+        return [pltpu.make_async_copy(w, buf.at[tile % 2], sems.at[j, tile % 2]) for j, (w, buf) in enumerate(pairs)]
+
+    def top_tile(tile):
+        rows = rows_at(tile * UT, UT, UT)
+        return [*tile_of(3, tile), pltpu.make_async_copy(wholes[5].at[rows], wd.at[rows], sems.at[2, tile % 2])]
+
+    fetch_down = lambda: pltpu.make_async_copy(wholes[2], wd, one_sem.at[0])
+    fetch_x = lambda: pltpu.make_async_copy(x, states, one_sem.at[1])
+    fetch_dy = lambda: pltpu.make_async_copy(dy, states, one_sem.at[2])
+
+    def start(copies):
+        for c in copies:
+            c.start()
+
+    def wait(copies):
+        for c in copies:
+            c.wait()
 
     @pl.when(step == 0)
     def _():
-        for c in fetch(0):
-            c.start()
+        start([*tile_of(0, 0), fetch_x()])
+        fetch_x().wait()
 
         def one(m):
-            a[m, :] = norm_tile(x[m, :])
+            a[m, :] = norm_tile(states[m, :])
 
         chunks(T, 256, one)
 
     @pl.when(step < UPS)
     def _():
-        for c in fetch(step):
-            c.wait()
+        wait(tile_of(0, step))
 
         @pl.when(step < UPS - 1)
         def _():
-            for c in fetch(step + 1):
-                c.start()
+            start(tile_of(0, step + 1))
 
         @pl.when(step == UPS - 1)
         def _():
@@ -408,22 +445,47 @@
         def one(m):
             g, u = dot(a[m, :], g_buf[step % 2]), dot(a[m, :], u_buf[step % 2])
             gate[m, :], up[m, :] = g, u
-            made = (g * jax.nn.sigmoid(g) * u).astype(BF)
-            hidden[m, :] = made
-            kept[m, rows_at(step * UT, UT, UT)] = made
-
-        chunks(T, MC, one)
+            product = (g * jax.nn.sigmoid(g) * u).astype(BF)
+            hidden[m, :] = product
+            kept[m, rows_at(step * UT, UT, UT)] = product
+
+        chunks(T, 1024, one)
 
     @pl.when(step == UPS)
     def _():
         fetch_down().wait()
 
-    @pl.when(step >= UPS)
+    @pl.when((step >= UPS) & (step < TOP))
     def _():
         m = rows_at((step - UPS) * TM, TM, TM)
-        new = x[m, :] + dot(kept[m, :], wd[...]).astype(BF)
+        new = states[m, :] + dot(kept[m, :], wd[...]).astype(BF)
         h[...] = new
-        a1[...] = norm_tile(new)
+        a1[m, :] = norm_tile(new)
+
+    @pl.when(step == TOP)
+    def _():
+        start([*top_tile(0), fetch_dy()])
+        fetch_dy().wait()
+
+    @pl.when(step >= TOP)
+    def _():
+        tile = step - TOP
+        wait(top_tile(tile))
+
+        @pl.when(tile < UPS - 1)
+        def _():
+            start(top_tile(tile + 1))
+
+        down = rows_at(tile * UT, UT, UT)
+
+        def one(m):
+            g, u = dot(a1[m, :], g_buf[tile % 2]), dot(a1[m, :], u_buf[tile % 2])
+            dh = dot(states[m, :], wd[down, :], 1, 1).astype(BF).astype(F32)
+            made[m, :] = (g * jax.nn.sigmoid(g) * u).astype(BF)
+            dgate[m, :], dup[m, :] = gates(g, u, dh)
+
+        chunks(T, 1024, one)
+        td[...] = dot(made[...], states[...], 0, 0).astype(BF)
 
 
 def gates(g, u, dh):
@@ -431,26 +493,11 @@
     return (dh * u * (sig * (1 + g * (1 - sig)))).astype(BF), (dh * (g * sig)).astype(BF)
 
 
-def top_body(a, dy, wg, wu, wd, hidden, dgate, dup):
-    def one(m):
-        g, u = dot(a[m, :], wg[...]), dot(a[m, :], wu[...])
-        dh = dot(dy[m, :], wd[...], 1, 1).astype(BF).astype(F32)
-        hidden[m, :] = (g * jax.nn.sigmoid(g) * u).astype(BF)
-        dgate[m, :], dup[m, :] = gates(g, u, dh)
-
-    chunks(T, MC, one)
-
-
-def wdown_body(hidden, dy, out):
-    out[...] = dot(hidden[...], dy[...], 0, 0).astype(BF)
-
-
 def low_body(dy, wd, gate, up, hidden, dgate, dup, out):
-    def one(m):
+    for k in range(T // 256):
+        m = pl.ds(k * 256, 256)
         dh = dot(dy[m, :], wd[...], 1, 1).astype(BF).astype(F32)
         dgate[m, :], dup[m, :] = gates(gate[m, :], up[m, :], dh)
-
-    chunks(T, MC, one)
     out[...] = dot(hidden[...], dy[...], 0, 0).astype(BF)
 
 
@@ -466,39 +513,60 @@
     ou[...] = dot(at[...], dup[...]).astype(BF)
 
 
-def back_body(dgate, dup, wg, wu, h, dy, out):
-    da = dot(dgate[...], wg[...], 1, 1) + dot(dup[...], wu[...], 1, 1)
-    wide = h[...].astype(F32)
+def back_loads(wg, wu, gs, us, sems):
+    out = []
+    for k in range(4):
+        c = pl.ds(k * D, D)
+        out.append([pltpu.make_async_copy(w.at[:, c], v.at[:, c], sems.at[j, k]) for j, (w, v) in enumerate(((wg, gs), (wu, us)))])
+    return out
+
+
+def back_early(dgate, dup, wg, wu, h, dy, out, gs, us, da, sems):
+    for pair in back_loads(wg, wu, gs, us, sems):
+        for c in pair:
+            c.start()
+
+
+def back_body(dgate, dup, wg, wu, h, dy, out, gs, us, da, sems):
+    first = pl.program_id(0) == 0
+
+    @pl.when(first)
+    def _():
+        for k, pair in enumerate(back_loads(wg, wu, gs, us, sems)):
+            for c in pair:
+                c.wait()
+            c = pl.ds(k * D, D)
+            more = dot(dgate[:, c], gs[:, c], 1, 1) + dot(dup[:, c], us[:, c], 1, 1)
+            da[...] = more if k == 0 else da[...] + more
+
+    @pl.when(jnp.logical_not(first))
+    def _():
+        da[...] = dot(dgate[...], gs[...], 1, 1) + dot(dup[...], us[...], 1, 1)
+
+    wide, total = h[...].astype(F32), da[...]
     scale = lax.rsqrt(jnp.mean(wide * wide, -1, keepdims=True) + 1e-6)
-    inner = jnp.mean(da * wide, -1, keepdims=True)
-    dh = scale * da - wide * (scale * scale * scale * inner)
+    inner = jnp.mean(total * wide, -1, keepdims=True)
+    dh = scale * total - wide * (scale * scale * scale * inner)
     out[...] = (dy[...].astype(F32) + dh.astype(BF).astype(F32)).astype(BF)
 
 
-def k_first(number, x, gather):
+def k_first(number, x, dy, gather):
     wide = pl.BlockSpec((T, UT), lambda i: (0, jnp.minimum(i, UPS - 1)))
-    r = pl.BlockSpec((TM, D), lambda i: (jnp.maximum(i - UPS, 0), 0))
+    late = pl.BlockSpec((T, UT), lambda i: (0, jnp.maximum(i - TOP, 0)))
+    r = pl.BlockSpec((TM, D), lambda i: (jnp.clip(i - UPS, 0, DOWNS - 1), 0))
     outs = [(resident((T, D)), sds((T, D))), (wide, sds((T, FF), F32)), (wide, sds((T, FF), F32)), (wide, sds((T, FF)))]
-    outs += [(r, sds((T, D))), (r, sds((T, D)))]
-    scratch = [pltpu.VMEM((2, D, UT), BF), pltpu.VMEM((2, D, UT), BF), pltpu.VMEM((T, FF), BF), pltpu.VMEM((FF, D), BF), DMA((2, 2)), DMA((1,))]
-    return call(number, first_body, UPS + T // TM, [resident((T, D))], outs, (x,), scratch, comms=[gather], share=True)
-
-
-def k_top(number, a, dy, wg, wu, wd, comms):
-    wide = columns(T, TN)
-    ins = [resident((T, D)), resident((T, D)), columns(D, TN), columns(D, TN), rows_of(TN, D)]
-    return call(number, top_body, FF // TN, ins, [(wide, sds((T, FF)))] * 3, (a, dy, wg, wu, wd), comms=comms)
-
-
-def k_wdown(number, hidden, dy, comms):
-    return call(number, wdown_body, FF // TN, [columns(T, TN), resident((T, D))], [(rows_of(TN, D), sds((FF, D)))], (hidden, dy), comms=comms)
+    outs += [(r, sds((T, D))), (resident((T, D)), sds((T, D))), (late, sds((T, FF))), (late, sds((T, FF)))]
+    outs += [(pl.BlockSpec((UT, D), lambda i: (jnp.maximum(i - TOP, 0), 0)), sds((FF, D)))]
+    scratch = [pltpu.VMEM((2, D, UT), BF), pltpu.VMEM((2, D, UT), BF), pltpu.VMEM((T, FF), BF), pltpu.VMEM((FF, D), BF)]
+    scratch += [pltpu.VMEM((T, D), BF), pltpu.VMEM((T, UT), BF), DMA((3, 2)), DMA((3,))]
+    return call(number, first_body, TOP + UPS, [ANY, ANY], outs, (x, dy), scratch, comms=[gather], share=True)
 
 
 def k_low(number, dy, wd, gate, up, hidden, comms):
-    wide = columns(T, TN)
-    ins = [resident((T, D)), rows_of(TN, D), wide, wide, wide]
-    outs = [(wide, sds((T, FF))), (wide, sds((T, FF))), (rows_of(TN, D), sds((FF, D)))]
-    return call(number, low_body, FF // TN, ins, outs, (dy, wd, gate, up, hidden), comms=comms)
+    wide = columns(T, UT)
+    ins = [resident((T, D)), rows_of(UT, D), wide, wide, wide]
+    outs = [(wide, sds((T, FF))), (wide, sds((T, FF))), (rows_of(UT, D), sds((FF, D)))]
+    return call(number, low_body, UPS, ins, outs, (dy, wd, gate, up, hidden), comms=comms)
 
 
 def k_wide(number, a, dgate, dup, comms):
@@ -509,34 +577,33 @@
 
 def k_back(number, dgate, dup, wg, wu, h, dy, comms):
     r = rows_of(TM, D)
-    ins = [rows_of(TM, FF), rows_of(TM, FF), resident((D, FF)), resident((D, FF)), r, r]
-    return call(number, back_body, T // TM, ins, [(r, sds((T, D)))], (dgate, dup, wg, wu, h, dy), comms=comms)
+    ins = [rows_of(TM, FF), rows_of(TM, FF), ANY, ANY, r, r]
+    scratch = [pltpu.VMEM((D, FF), BF), pltpu.VMEM((D, FF), BF), pltpu.VMEM((TM, D), F32), DMA((2, 4))]
+    outs = [(r, sds((T, D)))]
+    return call(number, back_body, T // TM, ins, outs, (dgate, dup, wg, wu, h, dy), scratch, comms=comms, early=back_early)
 
 
 def k_comm(number, comms):
     return call(number, None, 1, [], [], (), comms=comms)[1]
 
 
-SCATTER_AT = (0, 1, 2, 4, 8, 8, 8)
+SCATTER_AT = (0, 0.1, 1, 3, 8, 8, 8)
 CROSS_AT = (0, 6)
 
 
 def solution(mesh):
     def step(x, dy, wg, wu, wd):
         x, dy = x[0], dy[0]
-        when = (0, 0, 0, 0, 0, 3, 6, 9, 12, 15, 18, 21, 24, 24.1, 24.2)
-        gather = Gather([wg, wu, wd, wg, wu, wd], [0, 0, 0, 1, 1, 1], lambda k: when[k])
-        gather.reorder([(0, 0), (1, 0), (0, 1), (1, 1), *[(i, k) for i in range(2, 6) for k in range(2)]])
-        (a0, gate, up, hidden, h1, a1), (wg0, wu0, wd0, wg1, wu1, wd1) = k_first(0, x, gather)
-        (top, dgate, dup), _ = k_top(3, a1, dy, wg1, wu1, wd1, [])
-        (td1,), _ = k_wdown(4, top, dy, [])
+        work, when = gather_times()
+        gather = Gather([wg, wu, wd, wg, wu, wd], [0, 0, 0, 1, 1, 1], when).reorder(work)
+        (a0, gate, up, hidden, h1, a1, dgate, dup, td1), (wg0, wu0, wd0, wg1, wu1, wd1) = k_first(0, x, dy, gather)
         (tg1, tu1), (pd1,) = k_wide(5, a1, dgate, dup, [Scatter(td1, SCATTER_AT)])
         (dh,), (pg1, od1) = k_back(6, dgate, dup, wg1, wu1, h1, dy, [Scatter(tg1, SCATTER_AT), Cross(pd1, CROSS_AT)])
-        (dgate, dup, td0), (pu1, og1) = k_low(7, dh, wd0, gate, up, hidden, [Scatter(tu1, SCATTER_AT), Cross(pg1, CROSS_AT)])
+        (dgate, dup, td0), (pu1, og1) = k_low(7, dh, wd0, gate, up, hidden, [Scatter(tu1, (0, 0.1, 1, 6, 14, 16, 16)), Cross(pg1, (0, 10))])
         (tg0, tu0), (pd0, ou1) = k_wide(8, a0, dgate, dup, [Scatter(td0, SCATTER_AT), Cross(pu1, CROSS_AT)])
         last = [
             Cross(pd0, CROSS_AT),
-            Scatter(tg0, (0, 1, 1.1, 3, 7, 8.25, 8.7), True),
+            Scatter(tg0, (0, 0.1, 1, 3, 7, 8.25, 8.7), True),
             Scatter(tu0, (1.2, 4, 4.1, 8, 8.2, 8.4, 8.8), True, (0, 2)),
             Scatter(tu0, (2, 5, 8.05, 8.1, 8.3, 8.5, 8.9), True, (1, 2)),
         ]

time: 593 us -> 590 us (level); the launches traced: 593 us -> 584 us
  Pallas kernels: 582 us -> 572 us
    pallas_call x8 -> x6, Pallas kernels: 582 us -> 572 us  [call(): pl.pallas_call(kernel, grid=(steps,), in_specs=[*ins, *[ANY] * len(c_args...]
where the time goes in v3:
time: 590 us; the launch traced here: 584 us
  Pallas kernels  572 us (97%)
  other arithmetic  7.18 us (1%)
    pallas_call x6, Pallas kernels, call(): pl.pallas_call(kernel, grid=(steps,), in_specs=[*ins, *[ANY] * len(c_args...  572 us

profile of v3, /device:TPU:0, one launch (start us, length us, event | category | flops | bytes accessed | tf_op | source)
XLA Modules:
  0.0 583.9 jit_solution(6201404840336243989)
XLA Ops:
  0.6 253.1 %shard_map.84 = (bf16[2048,1024]{1,0:T(8,128)(2,1)}, f32[2048,4096]{1,0:T(8,128)}, f32[2048,4096]{1,0:T(8,128)}, bf16[2048,4096]{1,0:T(8,128)(2,1)}, bf16[2048,1...) custom-call(bf16[2048,1024]{1,0:T(8,128)(2,1)} %bitcast.12, ...), custom_call_target="tpu_custom_call" | custom-call | tf_op jit(solution)/shard_map/pallas_call | solution.py:376
  253.7 48.5 %shard_map.85 = (bf16[1024,4096]{1,0:T(8,128)(2,1)}, bf16[1024,4096]{1,0:T(8,128)(2,1)}, bf16[512,1024]{1,0:T(8,128)(2,1)}) custom-call(bf16[2048,1024]{1,0:T(8,128)(2,1)} %get-tuple-element.43.refs_0_, bf16[2048,4096]{1,0:T(8,128)(2,1)} %get-tuple-element.38.refs_1_.refs_0_, bf16[2048,4096]{1,0:T(8,128)(2,1)} %get-tuple-element.39.refs_2_.refs_1_, ...), custom_call_target="tpu_custom_call" | custom-call | tf_op jit(solution)/shard_map/pallas_call | solution.py:376
  302.2 55.0 %shard_map.86 = (bf16[2048,1024]{1,0:T(8,128)(2,1)}, bf16[128,4096]{1,0:T(8,128)(2,1)}, bf16[512,1024]{1,0:T(8,128)(2,1)}) custom-call(bf16[2048,4096]{1,0:T(8,128)(2,1)} %get-tuple-element.38.refs_1_.refs_0_, bf16[2048,4096]{1,0:T(8,128)(2,1)} %get-tuple-element.39.refs_2_.refs_1_, bf16[1024,4096]{1,0:T(8,128)(2,1)} %get-tuple-element.40.refs_2_, ...), custom_call_target="tpu_custom_call" | custom-call | tf_op jit(solution)/shard_map/pallas_call | solution.py:376
  357.2 67.2 %shard_map.87 = (bf16[2048,4096]{1,0:T(8,128)(2,1)}, bf16[2048,4096]{1,0:T(8,128)(2,1)}, bf16[4096,1024]{1,0:T(8,128)(2,1)}, bf16[128,4096]{1,0:T(8,128)(2,1)}, bf16[128,4096]{1,0:T(8,128)(2,1)}) custom-call(bf16[2048,1024]{1,0:T(8,128)(2,1)} %get-tuple-element.47.refs_0_.refs_5_, bf16[4096,1024]{1,0:T(8,128)(2,1)} %get-tuple-element.48.refs_1_, ...), custom_call_target="tpu_custom_call" | custom-call | tf_op jit(solution)/shard_map/pallas_call | solution.py:376
  424.4 50.4 %shard_map.88 = (bf16[1024,4096]{1,0:T(8,128)(2,1)}, bf16[1024,4096]{1,0:T(8,128)(2,1)}, bf16[512,1024]{1,0:T(8,128)(2,1)}, bf16[128,4096]{1,0:T(8,128)(2,1)}) custom-call(bf16[2048,1024]{1,0:T(8,128)(2,1)} %get-tuple-element.58.refs_0_, bf16[2048,4096]{1,0:T(8,128)(2,1)} %get-tuple-element.54.refs_1_.refs_0_, ...), custom_call_target="tpu_custom_call" | custom-call | tf_op jit(solution)/shard_map/pallas_call | solution.py:376
  474.8 98.0 %shard_map.89 = (bf16[2048,1024]{1,0:T(8,128)(2,1)}, bf16[512,1024]{1,0:T(8,128)(2,1)}, bf16[128,4096]{1,0:T(8,128)(2,1)}, bf16[128,2048]{1,0:T(8,128)(2,1)}, bf16[128,2048]{1,0:T(8,128)(2,1)}) custom-call(bf16[2048,4096]{1,0:T(8,128)(2,1)} %get-tuple-element.54.refs_1_.refs_0_, bf16[2048,4096]{1,0:T(8,128)(2,1)} %get-tuple-element.55.refs_2_.refs_1_, ...), custom_call_target="tpu_custom_call" | custom-call | tf_op jit(solution)/shard_map/pallas_call | solution.py:376
  572.8 1.3 maximum_bitcast_fusion
  574.1 0.0 copy-start.1
  574.1 0.0 copy-start.2
  574.1 4.4 pad_maximum_fusion
  578.5 0.0 copy-start
  578.5 0.0 copy-done.1
  578.5 0.0 copy-done.2
  578.6 1.5 pad_maximum_fusion.2
  580.1 1.4 copy-done
  581.5 2.0 copy.10
Async XLA Ops:
  574.1 4.4 copy-start.1
  574.1 4.4 copy-start.2
  578.5 2.9 copy-start
